TPU v7x, 32 devices: a whole 2x2x4 slice. The times are simulated.
32 devices in a mesh: grp: 4 (over z), pen: 8 (over y, x, core).
Axes of the slice: x: 2, y: 2, z: 4, core: 2. Of those that a mesh axis runs over, the one named last changes fastest.
Arguments:
- cell_offsets: int32 [2, 1048576], P(None, ('grp', 'pen')), may hold values from 0 to 1
- cell_z: int32 [1048576], P(('grp', 'pen')), may hold values from 0 to 255
- frac: float32 [3, 1048576], P(None, ('grp', 'pen')), may hold values from 0 to 1
- charges: float32 [1048576], P(('grp', 'pen')), may hold values from -4 to 4
- tile_counts: int32 [16384], P(('grp', 'pen')), may hold values from 16 to 64, as said below
Outputs:
- forces: float32 [3, 1048576], P(None, ('grp', 'pen'))
- energy: float32 [], replicated
Inputs may be any that keep to these rules, and one draw needn't show every extreme that they name: `tile_counts`: live slots of each tile; some tile holds 64.
All inputs are finite; a program needn't handle non-finite values.
Results may differ from a plain program's by a relative error of at most 0.0003.
Values sent between devices are 32-bit elements; how exact they have to be, the bound alone decides.
A program may use at most 256 MiB of HBM per device.

v0:
```python
import functools
import math

import jax
import jax.numpy as jnp
import numpy as np
from jax import lax
from jax.experimental import pallas as pl
from jax.experimental.pallas import tpu as pltpu
from jax.sharding import PartitionSpec as P

KX = 256
KY = 256
KZ = 256
ATOMS = 1048576


ewald_split = 0.6
highest = lax.Precision.HIGH


def shifted(block, axis, distance):
    devices = range(lax.axis_size(axis))
    route = [((i - distance) % len(devices), i) for i in devices]
    return lax.ppermute(block, axis, route)


def spline_rows(fracs):
    values = [jnp.ones_like(fracs)]
    fifth = values
    for order in range(2, 7):
        nxt = []
        for j in range(order):
            term = jnp.zeros_like(fracs)
            if j >= 1:
                term = values[j - 1] * (fracs + order - 1 - j)
            if j <= order - 2:
                term = term + values[j] * (1.0 - fracs + j)
            nxt.append(term / (order - 1))
        if order == 5:
            fifth = nxt
        values = nxt
    slopes = []
    for j in range(6):
        term = jnp.zeros_like(fracs)
        if j >= 1:
            term = fifth[j - 1]
        if j <= 4:
            term = term - fifth[j]
        slopes.append(term)
    return (values, slopes)


def select_rows(distance, values):
    total = jnp.zeros(distance.shape, jnp.float32)
    for j in range(6):
        total = jnp.where(distance == j, values[j], total)
    return total


def select_pair(distance, values, grades):
    total = jnp.zeros(distance.shape, jnp.float32)
    slope = jnp.zeros(distance.shape, jnp.float32)
    for j in range(6):
        hit = distance == j
        total = jnp.where(hit, values[j], total)
        slope = jnp.where(hit, grades[j], slope)
    return (total, slope)


def split(values):
    high = values.astype(jnp.bfloat16)
    low = (values - high.astype(jnp.float32)).astype(jnp.bfloat16)
    return (high, low)


def product(high, low, other, dims):
    other_high, other_low = split(other)
    rows = high.shape[0]
    both = lax.dot_general(
        jnp.concatenate([high, low], axis=0), other_high, dims, preferred_element_type=jnp.float32
    )
    rest = lax.dot_general(high, other_low, dims, preferred_element_type=jnp.float32)
    return both[:rows] + both[rows:] + rest


def row_of(values, i):
    return [value[i : i + 1] for value in values]


def y_offset(offset, slots):
    lane = lax.broadcasted_iota(jnp.int32, offset.shape, 1)
    return offset + 2 * (lane // slots)


def spread_kernel(per_row, slots, off_ref, z_ref, frac_ref, q_ref, grid_ref):
    width = z_ref.shape[1]
    size_z = grid_ref.shape[2]
    grid_ref[...] = jnp.zeros_like(grid_ref)

    def step(outer, carry):
        rows = pl.ds(pl.multiple_of(outer * 8, 8), 8)
        theta_x, _ = spline_rows(frac_ref[0, rows, :])
        theta_y, _ = spline_rows(frac_ref[1, rows, :])
        theta_z, _ = spline_rows(frac_ref[2, rows, :])
        charge = q_ref[rows, :]
        theta_x = [theta * charge for theta in theta_x]
        off_x = off_ref[0, rows, :]
        off_y = y_offset(off_ref[1, rows, :], slots)
        base = z_ref[rows, :]
        eight = lax.broadcasted_iota(jnp.int32, (8, width), 0)
        sixteen = lax.broadcasted_iota(jnp.int32, (16, width), 0)
        cells = lax.broadcasted_iota(jnp.int32, (size_z, width), 0)
        for i in range(8):
            weight_x = select_rows(eight - off_x[i : i + 1], row_of(theta_x, i))
            weight_y = select_rows(sixteen - off_y[i : i + 1], row_of(theta_y, i))
            weight_z = select_rows(
                (cells - base[i : i + 1]) & (size_z - 1), row_of(theta_z, i)
            )
            pair = jnp.concatenate([weight_x[k : k + 1] * weight_y for k in range(8)], axis=0)
            high, low = split(pair)
            out = product(high, low, weight_z, (((1,), (1,)), ((), ())))
            first = 2 * (outer * (8 // per_row) + i // per_row)
            y0 = 8 * (i % per_row)
            for k in range(8):
                grid_ref[first + k, y0 : y0 + 16, :] += out[16 * k : 16 * k + 16]
        return carry

    lax.fori_loop(0, z_ref.shape[0] // 8, step, 0)


def interp_kernel(
    per_row, slots, off_ref, z_ref, frac_ref, q_ref, pot_ref, up_ref, side_ref, out_ref, ext_ref
):
    width = z_ref.shape[1]
    size_z = pot_ref.shape[2]
    block_x, block_y = pot_ref.shape[0], pot_ref.shape[1]
    ext_ref[:block_x, :block_y] = pot_ref[...]
    ext_ref[block_x : block_x + 5, :block_y] = up_ref[...]
    ext_ref[block_x + 5 :, :block_y] = jnp.zeros((3, block_y, size_z), jnp.float32)
    ext_ref[: block_x + 5, block_y:] = side_ref[...]
    ext_ref[block_x + 5 :, block_y:] = jnp.zeros((3, 8, size_z), jnp.float32)

    def step(outer, carry):
        rows = pl.ds(pl.multiple_of(outer * 8, 8), 8)
        theta_x, slope_x = spline_rows(frac_ref[0, rows, :])
        theta_y, slope_y = spline_rows(frac_ref[1, rows, :])
        theta_z, slope_z = spline_rows(frac_ref[2, rows, :])
        off_x = off_ref[0, rows, :]
        off_y = y_offset(off_ref[1, rows, :], slots)
        base = z_ref[rows, :]
        eight = lax.broadcasted_iota(jnp.int32, (8, width), 0)
        sixteen = lax.broadcasted_iota(jnp.int32, (16, width), 0)
        cells = lax.broadcasted_iota(jnp.int32, (size_z, width), 0)
        dims = (((1,), (0,)), ((), ()))
        forces = [[], [], []]
        for i in range(8):
            weight_x, grade_x = select_pair(
                eight - off_x[i : i + 1], row_of(theta_x, i), row_of(slope_x, i)
            )
            weight_y, grade_y = select_pair(
                sixteen - off_y[i : i + 1], row_of(theta_y, i), row_of(slope_y, i)
            )
            weight_z, grade_z = select_pair(
                (cells - base[i : i + 1]) & (size_z - 1), row_of(theta_z, i), row_of(slope_z, i)
            )
            first = 2 * (outer * (8 // per_row) + i // per_row)
            y0 = 8 * (i % per_row)
            footing = jnp.concatenate(
                [ext_ref[first + k, y0 : y0 + 16, :] for k in range(8)], axis=0
            )
            high, low = split(footing)
            main = product(high, low, weight_z, dims)
            tilt = product(high, low, grade_z, dims)
            along_x = 0.0
            along_y = 0.0
            along_z = 0.0
            for k in range(8):
                piece = main[16 * k : 16 * k + 16]
                along_x = along_x + grade_x[k : k + 1] * piece
                along_y = along_y + weight_x[k : k + 1] * piece
                along_z = along_z + weight_x[k : k + 1] * tilt[16 * k : 16 * k + 16]
            forces[0].append(jnp.sum(along_x * weight_y, axis=0, keepdims=True))
            forces[1].append(jnp.sum(along_y * grade_y, axis=0, keepdims=True))
            forces[2].append(jnp.sum(along_z * weight_y, axis=0, keepdims=True))
        minus_q = -q_ref[rows, :]
        for d in range(3):
            out_ref[d, rows, :] = minus_q * jnp.concatenate(forces[d], axis=0)
        return carry

    lax.fori_loop(0, z_ref.shape[0] // 8, step, 0)


def modulus(index, length):
    coeffs = (1.0 / 120.0, 26.0 / 120.0, 66.0 / 120.0, 26.0 / 120.0, 1.0 / 120.0)
    real_part = 0.0
    imag_part = 0.0
    for j in range(5):
        angle = (index * j % length).astype(jnp.float32) * (2.0 * math.pi / length)
        real_part = real_part + coeffs[j] * jnp.cos(angle)
        imag_part = imag_part + coeffs[j] * jnp.sin(angle)
    return real_part * real_part + imag_part * imag_part


def influence(index_x, index_y, index_z):
    freq_x = jnp.where(2 * index_x < KX, index_x, index_x - KX).astype(jnp.float32) / KX
    freq_y = jnp.where(2 * index_y < KY, index_y, index_y - KY).astype(jnp.float32) / KY
    freq_z = jnp.where(2 * index_z < KZ, index_z, index_z - KZ).astype(jnp.float32) / KZ
    square = freq_x * freq_x + freq_y * freq_y + freq_z * freq_z
    safe = jnp.where(square > 0, square, 1.0)
    volume = float(KX * KY * KZ)
    value = jnp.exp(-math.pi**2 * safe / ewald_split**2) / (math.pi * volume * safe)
    value = value / (modulus(index_x, KX) * modulus(index_y, KY) * modulus(index_z, KZ))
    return jnp.where(square > 0, value, 0.0)


def waves(index, length):
    angle = (index % length) * (2.0 * math.pi / length)
    return (np.cos(angle), np.sin(angle))


def z_table(groups):
    planes = KZ // (2 * groups)
    frequency = np.arange(KZ // 2).reshape(groups, planes)
    cos, sin = waves(frequency[..., None] * np.arange(KZ), KZ)
    table = np.stack([cos, -sin], axis=1)
    table[0, 1, 0] = waves(np.arange(KZ) * (KZ // 2), KZ)[0]
    weight = np.full((groups, 2, planes), 2.0)
    weight[0, :, 0] = 1.0
    table = table.reshape(KZ, KZ)
    return (table.astype(np.float32), (table * weight.reshape(KZ, 1)).astype(np.float32))


def block_table(frequency, length, groups):
    position = np.arange(length)
    cos, sin = waves(frequency[..., None] * position, length)
    shape = (frequency.shape[0], frequency.shape[1], groups, length // groups)
    cos, sin = cos.reshape(shape), sin.reshape(shape)
    real_row = np.stack([cos, sin], axis=3)
    imag_row = np.stack([-sin, cos], axis=3)
    table = np.stack([real_row, imag_row], axis=1)
    return table.reshape(2 * length, 2 * length).astype(np.float32)


def y_frequency(groups):
    first = np.arange(KY // 2).reshape(groups, -1)
    second = np.where(first == 0, KY // 2, (KY - first) % KY)
    return np.concatenate([first, second], axis=1)


def partner_of(me, d, count):
    if count & (count - 1):
        return lax.rem(me + d, count)
    peer = me
    bit = 1
    while bit < count:
        if d & bit:
            peer = peer + bit - 2 * bit * lax.rem(lax.div(me, bit), 2)
        bit = 2 * bit
    return peer


def exchange_kernel(axis, count, *refs):
    arrays = (len(refs) - 3) // 2
    sources, targets = refs[:arrays], refs[arrays : 2 * arrays]
    send_sem, recv_sem, own_sem = refs[2 * arrays :]
    me = lax.axis_index(axis)
    barrier = pltpu.get_barrier_semaphore()
    for d in range(1, count):
        pl.semaphore_signal(
            barrier,
            inc=1,
            device_id={axis: partner_of(me, d, count)},
            device_id_type=pl.DeviceIdType.MESH,
        )
    pl.semaphore_wait(barrier, count - 1)
    copies = []
    for k in range(arrays):
        for d in range(1, count):
            peer = partner_of(me, d, count)
            copies.append(
                pltpu.make_async_remote_copy(
                    src_ref=sources[k].at[peer],
                    dst_ref=targets[k].at[me],
                    send_sem=send_sem.at[k, d],
                    recv_sem=recv_sem.at[k, d],
                    device_id={axis: peer},
                    device_id_type=pl.DeviceIdType.MESH,
                )
            )
        copies.append(
            pltpu.make_async_copy(sources[k].at[me], targets[k].at[me], own_sem.at[k])
        )
    for copy in copies:
        copy.start()
    for copy in copies:
        copy.wait()


def exchange(arrays, axis, number):
    count = lax.axis_size(axis)
    vmem = pl.BlockSpec(memory_space=pltpu.VMEM)
    return pl.pallas_call(
        functools.partial(exchange_kernel, axis, count),
        out_shape=[jax.ShapeDtypeStruct(array.shape, array.dtype) for array in arrays],
        in_specs=[vmem] * len(arrays),
        out_specs=[vmem] * len(arrays),
        scratch_shapes=[
            pltpu.SemaphoreType.DMA((len(arrays), count)),
            pltpu.SemaphoreType.DMA((len(arrays), count)),
            pltpu.SemaphoreType.DMA((len(arrays),)),
        ],
        compiler_params=pltpu.CompilerParams(collective_id=number, has_side_effects=True),
        name="exchange" + str(number),
    )(*arrays)


def dot(left, right, left_dim, right_dim):
    dims = (((left_dim,), (right_dim,)), ((), ()))
    return lax.dot_general(
        left, right, dims, precision=highest, preferred_element_type=jnp.float32
    )


def spectrum_of(grid, block_x, block_y):
    grp, pen = lax.axis_size("grp"), lax.axis_size("pen")
    planes = KZ // (2 * pen)
    lines = KY // grp
    half = lines // 2
    forward_z, backward_z = z_table(pen)
    order_y = y_frequency(grp)
    table_y = block_table(order_y, KY, pen)
    table_x = block_table(np.arange(KX)[None], KX, grp)
    lines_z = dot(forward_z, grid.reshape(block_x * block_y, KZ), 1, 1)
    lines_z = lines_z.reshape(pen, 2, planes, block_x, block_y).transpose(0, 1, 4, 2, 3)
    (columns,) = exchange(
        [lines_z.reshape(pen, 2 * block_y, planes * block_x)], "pen", 1
    )
    lines_y = dot(table_y, columns.reshape(2 * KY, planes * block_x), 1, 0)
    lines_y = lines_y.reshape(grp, 2, lines, planes, block_x).transpose(0, 1, 4, 3, 2)
    (rows,) = exchange([lines_y.reshape(grp, 2 * block_x, planes * lines)], "grp", 2)
    rows = rows.reshape(grp, 2, block_x, planes * lines)
    at_grp, at_pen = lax.axis_index("grp"), lax.axis_index("pen")
    packed = rows[..., :lines]
    alone = (at_grp == 0) & (jnp.arange(lines) % half == 0)
    partner = jnp.where(
        alone, packed, jnp.concatenate([packed[..., half:], packed[..., :half]], axis=-1)
    )
    a, b = packed[:, :1], packed[:, 1:]
    c, d = partner[:, :1], partner[:, 1:]
    whole = jnp.concatenate([a + c, b - d], axis=1) * 0.5
    midway = jnp.concatenate([b + d, c - a], axis=1) * 0.5
    origin = at_pen == 0
    whole = jnp.where(origin, whole, packed)
    midway = jnp.where(origin, midway, 0.0)
    total_lanes = (planes + 1) * lines
    full = jnp.concatenate([whole, rows[..., lines:], midway], axis=-1)
    spectrum = dot(table_x, full.reshape(2 * KX, total_lanes), 1, 0)
    spectrum = spectrum.reshape(2, KX, total_lanes)
    index_x = jnp.arange(KX, dtype=jnp.int32)[:, None]
    slot = jnp.arange(planes + 1, dtype=jnp.int32)
    index_z = jnp.where(slot < planes, at_pen * planes + slot, KZ // 2)
    plane_weight = jnp.where(
        slot < planes,
        jnp.where(origin & (slot == 0), 1.0, 2.0),
        jnp.where(origin, 1.0, 0.0),
    )
    index_z = jnp.repeat(index_z, lines)[None, :]
    plane_weight = jnp.repeat(plane_weight, lines)[None, :]
    index_y = lax.dynamic_index_in_dim(jnp.asarray(order_y, jnp.int32), at_grp, 0, False)
    index_y = jnp.tile(index_y, planes + 1)[None, :]
    kernel = influence(index_x, index_y, index_z)
    power = spectrum[0] * spectrum[0] + spectrum[1] * spectrum[1]
    spectral = 0.5 * jnp.sum(plane_weight * kernel * power)
    scaled = (spectrum * kernel).reshape(2 * KX, total_lanes)
    returning = dot(table_x, scaled, 0, 0).reshape(grp, 2, block_x, total_lanes)
    midway = returning[..., planes * lines :]
    turned = jnp.concatenate([-midway[:, 1:], midway[:, :1]], axis=1)
    returning = jnp.concatenate(
        [returning[..., :lines] + turned, returning[..., lines : planes * lines]], axis=-1
    )
    rows, sums = exchange(
        [
            returning.reshape(grp, 2 * block_x, planes * lines),
            jnp.broadcast_to(spectral, (grp, 8, 128)),
        ],
        "grp",
        3,
    )
    spectral = jnp.sum(sums[:, 0, 0])
    rows = rows.reshape(grp, 2, block_x, planes, lines).transpose(0, 1, 4, 3, 2)
    columns = dot(table_y, rows.reshape(2 * KY, planes * block_x), 0, 0)
    columns, sums = exchange(
        [
            columns.reshape(pen, 2 * block_y, planes * block_x),
            jnp.broadcast_to(spectral, (pen, 8, 128)),
        ],
        "pen",
        4,
    )
    spectral = jnp.sum(sums[:, 0, 0])
    home = columns.reshape(pen, 2, block_y, planes, block_x).transpose(0, 1, 3, 4, 2)
    potential = dot(home.reshape(KZ, block_x * block_y), backward_z, 0, 0)
    return (potential.reshape(block_x, block_y, KZ), spectral)


def local(cell_offsets, cell_z, frac, charges, tile_counts):
    block_x = KX // lax.axis_size("grp")
    block_y = KY // lax.axis_size("pen")
    tiles = tile_counts.shape[0]
    slots = charges.shape[0] // tiles
    width = 4 * slots
    groups = tiles // 4
    per_row = block_y // 8
    live = jnp.arange(slots, dtype=jnp.int32)[None, :] < tile_counts[:, None]
    live_q = (charges.reshape(tiles, slots) * live.astype(jnp.float32)).reshape(groups, width)
    offsets = cell_offsets.reshape(2, groups, width)
    zcell = cell_z.reshape(groups, width)
    fracs = frac.reshape(3, groups, width)
    vmem = pl.BlockSpec(memory_space=pltpu.VMEM)
    params = pltpu.CompilerParams(vmem_limit_bytes=60 * 1024 * 1024)
    padded = pl.pallas_call(
        functools.partial(spread_kernel, per_row, slots),
        out_shape=jax.ShapeDtypeStruct((block_x + 8, block_y + 8, KZ), jnp.float32),
        in_specs=[vmem] * 4,
        out_specs=vmem,
        compiler_params=params,
        name="spread",
    )(offsets, zcell, fracs, live_q)
    rim_y = shifted(padded[: block_x + 5, block_y : block_y + 5], "pen", 1)
    merged = padded[: block_x + 5, :block_y].at[:, :5].add(rim_y)
    rim_x = shifted(merged[block_x : block_x + 5], "grp", 1)
    grid = merged[:block_x] + jnp.pad(rim_x, ((0, block_x - 5), (0, 0), (0, 0)))
    potential, total = spectrum_of(grid, block_x, block_y)
    upper = shifted(potential[:5], "grp", -1)
    ext_x = jnp.concatenate([potential[:, :5], upper[:, :5]], axis=0)
    beside = shifted(ext_x, "pen", -1)
    beside = jnp.pad(beside, ((0, 0), (0, 3), (0, 0)))
    forces = pl.pallas_call(
        functools.partial(interp_kernel, per_row, slots),
        out_shape=jax.ShapeDtypeStruct((3, groups, width), jnp.float32),
        in_specs=[vmem] * 7,
        out_specs=vmem,
        scratch_shapes=[pltpu.VMEM((block_x + 8, block_y + 8, KZ), jnp.float32)],
        compiler_params=params,
        name="interp",
    )(offsets, zcell, fracs, live_q, potential, upper, beside)
    return (forces.reshape(3, groups * width), total / ATOMS)


def solution(mesh):
    in_specs = (
        P(None, ("grp", "pen")),
        P(("grp", "pen")),
        P(None, ("grp", "pen")),
        P(("grp", "pen")),
        P(("grp", "pen")),
    )
    out_specs = (P(None, ("grp", "pen")), P())
    return jax.shard_map(local, mesh=mesh, in_specs=in_specs, out_specs=out_specs, check_vma=False)
```

profile of v0, /device:TPU:1, one launch (start us, length us, event | category | flops | bytes accessed | tf_op | source)
XLA Modules:
  0.0 398.0 jit_solution(3348445581349137916)
XLA Ops:
  7.6 33.2 %spread.1 = f32[72,40,256]{2,1,0:T(8,128)} custom-call(s32[2,128,256]{2,1,0:T(8,128)} %bitcast.72, s32[128,256]{1,0:T(8,128)} %reshape.776.z_ref, f32[3,128,256]{2,1,0:T(8,128)} %bitcast.70, f32[128,256]{1,0:T(8,128)} %compare_select_fusion.2.q_ref), custom_call_target="tpu_custom_call" | custom-call | tf_op jit(solution)/shard_map/spread/pallas_call | solution.py:422
  50.3 5.7 %scatter-add.4 = f32[69,32,256]{2,1,0:T(8,128)S(1)} dynamic-update-slice(f32[69,32,256]{2,1,0:T(8,128)S(1)} %slice.133, f32[69,5,256]{2,1,0:T(8,128)S(1)} %slice_add_fusion.1, s32[]{:T(128)} %constant.221.clone.1, s32[]{:T(128)} %constant.221.clone.1, s32[]{:T(128)} %constant.221.clone.1) | dynamic-update-slice | bytes 706564 | tf_op jit(solution)/shard_map/scatter-add | solution.py:431
  57.8 4.5 %collective-permute-done.1 = f32[5,32,256]{2,1,0:T(8,128)S(1)} collective-permute-done((f32[5,32,256]{2,1,0:T(8,128)S(1)}, f32[5,32,256]{2,1,0:T(8,128)S(1)}, u32[]{:S(2)}, u32[]{:S(2)}) %collective-permute-start.1) | collective-permute-done | bytes 163872 | tf_op jit(solution)/shard_map/ppermute | solution.py:25
  63.6 4.8 %reshape.780 = f32[8,2,16,64,32]{4,3,2,1,0:T(8,128)} reshape(f32[256,2048]{1,0:T(8,128)S(1)} %fusion.59) | data formatting | bytes 4194304 | tf_op jit(solution)/shard_map/reshape | solution.py:335
  68.4 6.9 %copy.29 = f32[8,2,32,16,64]{4,3,2,1,0:T(8,128)} copy(f32[8,2,32,16,64]{2,4,3,1,0:T(8,128)} %bitcast.49) | data formatting | bytes 4194304 | tf_op jit(solution)/shard_map/transpose | solution.py:335
  75.3 4.8 %reshape.781.refs_0_ = f32[8,64,1024]{2,1,0:T(8,128)} reshape(f32[8,2,32,16,64]{4,3,2,1,0:T(8,128)} %copy.29) | data formatting | bytes 4194304 | tf_op jit(solution)/shard_map/reshape | solution.py:337
  80.1 32.3 %exchange1.1 = f32[8,64,1024]{2,1,0:T(8,128)} custom-call(f32[8,64,1024]{2,1,0:T(8,128)} %reshape.781.refs_0_), custom_call_target="tpu_custom_call" | custom-call | tf_op jit(solution)/shard_map/exchange1/pallas_call | solution.py:303
  112.4 3.4 fusion.60
  118.4 5.8 %copy.30 = f32[4,2,64,16,64]{2,3,4,1,0:T(8,128)} copy(f32[4,2,64,16,64]{4,3,2,1,0:T(8,128)} %reshape.783) | data formatting | bytes 4194304 | tf_op jit(solution)/shard_map/reshape | solution.py:340
  124.2 4.9 %reshape.784.refs_0_ = f32[4,128,1024]{2,1,0:T(8,128)} reshape(f32[4,2,64,16,64]{4,3,2,1,0:T(8,128)} %bitcast.51) | data formatting | bytes 4194304 | tf_op jit(solution)/shard_map/reshape | solution.py:341
  129.1 40.7 %exchange2.1 = f32[4,128,1024]{2,1,0:T(8,128)} custom-call(f32[4,128,1024]{2,1,0:T(8,128)} %reshape.784.refs_0_), custom_call_target="tpu_custom_call" | custom-call | tf_op jit(solution)/shard_map/exchange2/pallas_call | solution.py:303
  171.0 3.5 slice.145
  189.0 4.3 %fusion = f32[512,1088]{1,0:T(8,128)S(1)} fusion(f32[512,512]{1,0:T(8,128)S(1)} %copy-done.2, f32[512,1088]{0,1:T(8,128)S(1)} %fusion.61, f32[512,1088]{0,1:T(8,128)S(1)} %bitcast.64), kind=kOutput, calls=%fused_computation | convolution fusion | flops 1711833088 | bytes 7733248 | tf_op jit(solution)/shard_map/dot_general | solution.py:320
  197.2 59.7 %exchange3.1 = (f32[4,128,1024]{2,1,0:T(8,128)}, f32[4,8,128]{2,1,0:T(8,128)}) custom-call(f32[4,128,1024]{2,1,0:T(8,128)} %bitcast.66, f32[4,8,128]{2,1,0:T(8,128)} %broadcast_in_dim.54.refs_1_), custom_call_target="tpu_custom_call" | custom-call | tf_op jit(solution)/shard_map/exchange3/pallas_call | solution.py:303
  256.9 4.5 %reshape.789 = f32[4,2,64,16,64]{4,3,2,1,0:T(8,128)} reshape(f32[4,128,1024]{2,1,0:T(8,128)} %get-tuple-element.18) | data formatting | bytes 4194304 | tf_op jit(solution)/shard_map/reshape | solution.py:391
  261.4 5.8 %copy.32 = f32[4,2,64,16,64]{2,3,4,1,0:T(8,128)} copy(f32[4,2,64,16,64]{4,3,2,1,0:T(8,128)} %reshape.789) | data formatting | bytes 4194304 | tf_op jit(solution)/shard_map/reshape | solution.py:391
  267.2 3.5 reshape.790
  276.5 31.6 %exchange4.1 = (f32[8,64,1024]{2,1,0:T(8,128)}, f32[8,8,128]{2,1,0:T(8,128)}) custom-call(f32[8,64,1024]{2,1,0:T(8,128)} %bitcast.67, f32[8,8,128]{2,1,0:T(8,128)} %broadcast_in_dim.55.refs_1_), custom_call_target="tpu_custom_call" | custom-call | tf_op jit(solution)/shard_map/exchange4/pallas_call | solution.py:303
  308.2 4.5 %reshape.792 = f32[8,2,32,16,64]{4,3,2,1,0:T(8,128)} reshape(f32[8,64,1024]{2,1,0:T(8,128)} %get-tuple-element.20) | data formatting | bytes 4194304 | tf_op jit(solution)/shard_map/reshape | solution.py:402
  312.7 6.9 %copy.33 = f32[8,2,32,16,64]{2,4,3,1,0:T(8,128)} copy(f32[8,2,32,16,64]{4,3,2,1,0:T(8,128)} %reshape.792) | data formatting | bytes 4194304 | tf_op jit(solution)/shard_map/reshape | solution.py:402
  319.6 7.5 %reshape.793 = f32[256,2048]{1,0:T(8,128)} reshape(f32[8,2,16,64,32]{4,3,2,1,0:T(8,128)} %bitcast.50) | data formatting | bytes 4194304 | tf_op jit(solution)/shard_map/reshape | solution.py:403
  332.3 3.8 collective-permute-done.2.up_ref
  339.6 3.7 collective-permute-done.3
  344.2 50.6 %interp.1 = f32[3,128,256]{2,1,0:T(8,128)} custom-call(s32[2,128,256]{2,1,0:T(8,128)} %bitcast.73, s32[128,256]{1,0:T(8,128)} %reshape.776.z_ref, f32[3,128,256]{2,1,0:T(8,128)} %bitcast.71, f32[128,256]{1,0:T(8,128)} %compare_select_fusion.2.q_ref, f32[64,32,256]{2,1,0:T(8,128)} %bitcast.59, f32[5,32,256]{2,1,0:T(8,128)} %copy-done.5, ...), custom_call_target="tpu_custom_call" | custom-call | tf_op jit(solution)/shard_map/interp/pallas_call | solution.py:439
  (77 shorter events, 57.7 us)
Async XLA Ops:
  0.6 5.6 %copy-start.6 = (s32[32768]{0:T(1024)S(1)}, s32[32768]{0:T(1024)}, u32[]{:S(2)}) copy-start(s32[32768]{0:T(1024)} %param.13) | copy-start | bytes 393220
  42.0 7.1 %collective-permute-start = (f32[69,5,256]{2,0,1:T(8,128)S(1)}, f32[69,5,256]{2,0,1:T(8,128)S(1)}, u32[]{:S(2)}, u32[]{:S(2)}) collective-permute-start(f32[69,5,256]{2,0,1:T(8,128)S(1)} %copy.27), channel_id=1, source_target_pairs={{7,0},{0,1},{1,2},{2,3},{3,4},{4,5},{5,6},{6,7},{15,8},{8,9},{9,10... | collective-permute-start | bytes 1059848 | tf_op jit(solution)/shard_map/ppermute | solution.py:25
  56.0 6.3 %collective-permute-start.1 = (f32[5,32,256]{2,1,0:T(8,128)S(1)}, f32[5,32,256]{2,1,0:T(8,128)S(1)}, u32[]{:S(2)}, u32[]{:S(2)}) collective-permute-start(f32[5,32,256]{2,1,0:T(8,128)S(1)} %slice.137), channel_id=1, source_target_pairs={{24,0},{0,8},{8,16},{16,24},{25,1},{1,9},{9,17},{17,25},{26,2},{2,... | collective-permute-start | bytes 491528 | tf_op jit(solution)/shard_map/ppermute | solution.py:25
  57.8 4.7 %copy-start.4 = (f32[256,256]{1,0:T(8,128)S(1)}, f32[256,256]{1,0:T(8,128)}, u32[]{:S(2)}) copy-start(f32[256,256]{1,0:T(8,128)} %constant.244.clone) | copy-start | bytes 786436
  80.1 32.3 %copy-start.1 = (f32[512,512]{1,0:T(8,128)S(1)}, f32[512,512]{1,0:T(8,128)}, u32[]{:S(2)}) copy-start(f32[512,512]{1,0:T(8,128)} %constant.245.clone) | copy-start | bytes 3145732
  187.8 1.2 copy-start.2
  319.6 7.5 %copy-start.3 = (f32[256,256]{1,0:T(8,128)S(1)}, f32[256,256]{1,0:T(8,128)}, u32[]{:S(2)}) copy-start(f32[256,256]{1,0:T(8,128)} %constant.248.clone) | copy-start | bytes 786436
  330.6 12.8 %copy-start = (f32[2048,256]{1,0:T(8,128)}, f32[2048,256]{1,0:T(8,128)S(1)}, u32[]{:S(2)}) copy-start(f32[2048,256]{1,0:T(8,128)S(1)} %fusion.63) | copy-start | bytes 6291460
  330.6 5.4 %collective-permute-start.2 = (f32[5,32,256]{2,1,0:T(8,128)S(1)}, f32[5,32,256]{2,1,0:T(8,128)S(1)}, u32[]{:S(2)}, u32[]{:S(2)}) collective-permute-start(f32[5,32,256]{2,1,0:T(8,128)S(1)} %bitcast.79), channel_id=1, source_target_pairs={{8,0},{16,8},{24,16},{0,24},{9,1},{17,9},{25,17},{1,25},{10,2},{18... | collective-permute-start | bytes 491528 | tf_op jit(solution)/shard_map/ppermute | solution.py:25
  336.0 8.2 %copy-start.5 = (f32[5,32,256]{2,1,0:T(8,128)}, f32[5,32,256]{2,1,0:T(8,128)S(1)}, u32[]{:S(2)}) copy-start(f32[5,32,256]{2,1,0:T(8,128)S(1)} %collective-permute-done.2.up_ref) | copy-start | bytes 491524
  336.2 7.0 %collective-permute-start.3 = (f32[69,5,256]{2,0,1:T(8,128)S(1)}, f32[69,5,256]{2,0,1:T(8,128)S(1)}, u32[]{:S(2)}, u32[]{:S(2)}) collective-permute-start(f32[69,5,256]{2,0,1:T(8,128)S(1)} %copy.34), channel_id=1, source_target_pairs={{1,0},{2,1},{3,2},{4,3},{5,4},{6,5},{7,6},{0,7},{9,8},{10,9},{11,1... | collective-permute-start | bytes 1059848 | tf_op jit(solution)/shard_map/ppermute | solution.py:25
where the time goes:
time: 400 us; the launch traced here: 398 us
  Pallas kernels  248 us (62%)
  local copies, waits for them, and re-layouts  94.3 us (24%)
  matrix products  18.9 us (5%)
  waiting for transfers between devices  13.4 us (3%)
  other arithmetic  13 us (3%)
  starting transfers between devices  7.07 us (2%)
    pallas_call x4, Pallas kernels, exchange(): pl.pallas_call(functools.partial(exchange_kernel, axis, count), out_shape...  164 us
    pallas_call x1, Pallas kernels, local(): pl.pallas_call(functools.partial(interp_kernel, per_row, slots), out_shap...  50.6 us
    pallas_call x1, Pallas kernels, local(): pl.pallas_call(functools.partial(spread_kernel, per_row, slots), out_shap...  33.2 us
    dot_general x6, matrix products, dot(): lax.dot_general(left, right, dims, precision=highest, preferred_element_t...  18.9 us
    ppermute x4, waiting for transfers between devices, shifted(): return lax.ppermute(block, axis, route)  13.4 us
    reshape x2, local copies, waits for them, and re-layouts, spectrum_of(): columns.reshape(pen, 2, block_y, planes, block_x).transpose(0, 1, 3, 4, 2)  11.5 us
    reshape x2, local copies, waits for them, and re-layouts, spectrum_of(): rows = rows.reshape(grp, 2, block_x, planes, lines).transpose(0, 1, 4, 3, 2)  10.4 us
    reshape x2, local copies, waits for them, and re-layouts, spectrum_of(): lines_y.reshape(grp, 2, lines, planes, block_x).transpose(0, 1, 4, 3, 2)  8.37 us
  transfers between devices with their start and end apart: 4, of which 4 were waited for; matrix products, arithmetic and copies ran while one was open for 1% of the time, Pallas kernels for 0%

commit v1 on v0

--- a/solution.py
+++ b/solution.py
@@ -404,6 +404,251 @@
     return (potential.reshape(block_x, block_y, KZ), spectral)
 
 
+def cas_table(length):
+    position = np.arange(length)
+    cos, sin = waves(position[:, None] * position, length)
+    return cos + sin
+
+
+def halves(table):
+    high = table.astype(jnp.bfloat16)
+    low = (table - high.astype(np.float64)).astype(jnp.bfloat16)
+    return (high, low)
+
+
+def spline_factor(length):
+    index = np.arange(length)
+    freq = np.where(2 * index < length, index, index - length) / length
+    coeffs = np.array([1.0, 26.0, 66.0, 26.0, 1.0]) / 120.0
+    phase = np.exp(2j * np.pi * index[:, None] * np.arange(5) / length)
+    modulus_square = np.abs(phase @ coeffs) ** 2
+    square = freq**2
+    factor = np.exp(-(math.pi**2) * square / ewald_split**2) / modulus_square
+    return (factor.astype(np.float32), square.astype(np.float32))
+
+
+def dot3(left, right, left_dim, right_dim):
+    dims = (((left_dim,), (right_dim,)), ((), ()))
+    one = functools.partial(
+        lax.dot_general, dimension_numbers=dims, preferred_element_type=jnp.float32
+    )
+    return one(left[0], right[0]) + one(left[0], right[1]) + one(left[1], right[0])
+
+
+def regroup(tiles, width):
+    lane = lax.broadcasted_iota(jnp.int32, tiles[0].shape, 1) // width
+    bit = 1
+    while bit < len(tiles):
+        keep = (lane // bit) % 2 == 0
+        mixed = list(tiles)
+        for i in range(len(tiles)):
+            if not i & bit:
+                first, second = tiles[i], tiles[i + bit]
+                mixed[i] = jnp.where(keep, first, pltpu.roll(second, bit * width, 1))
+                mixed[i + bit] = jnp.where(
+                    keep, pltpu.roll(first, 128 - bit * width, 1), second
+                )
+        tiles = mixed
+        bit = 2 * bit
+    return tiles
+
+
+def slab_kernel(
+    grp, pen, grid_ref, cas_hi, cas_lo, into_hi, into_lo, back_hi, back_lo,
+    factor_row, factor_col, square_row, square_col, pot_ref, energy_ref,
+    send, recv, send_back, recv_back, work, sums, part,
+    send_sem, recv_sem, back_send_sem, back_recv_sem, sum_send_sem, sum_recv_sem,
+):
+    count = grp * pen
+    block_x, block_y = grid_ref.shape[0], grid_ref.shape[1]
+    fan = 128 // block_y
+    tiles = block_x // fan
+    half = pen // fan
+    at_grp, at_pen = lax.axis_index("grp"), lax.axis_index("pen")
+    me = at_grp * pen + at_pen
+
+    def peer_of(d):
+        peer = partner_of(me, d, count)
+        return (peer, {"grp": peer // pen, "pen": peer % pen})
+
+    barrier = pltpu.get_barrier_semaphore()
+    for d in range(1, count):
+        pl.semaphore_signal(
+            barrier, inc=1, device_id=peer_of(d)[1], device_id_type=pl.DeviceIdType.MESH
+        )
+    cas = (cas_hi[...], cas_lo[...])
+
+    def along_z(i, carry):
+        rows = grid_ref[pl.ds(2 * fan * i, 2 * fan)].reshape(256, KZ)
+        out = dot3(cas, split(rows), 1, 1)
+        for t in range(2):
+            send[:, 2 * i + t] = out[:, 128 * t : 128 * t + 128].reshape(count, 8, 128)
+        return carry
+
+    lax.fori_loop(0, tiles // 2, along_z, 0)
+    pl.semaphore_wait(barrier, count - 1)
+
+    def copy_of(d, source, target, sems):
+        peer, where = peer_of(d)
+        return pltpu.make_async_remote_copy(
+            src_ref=source(peer),
+            dst_ref=target.at[me],
+            send_sem=sems[0].at[d],
+            recv_sem=sems[1].at[d],
+            device_id=where,
+            device_id_type=pl.DeviceIdType.MESH,
+        )
+
+    out_copies = {
+        d: copy_of(d, lambda p: send.at[p], recv, (send_sem, recv_sem))
+        for d in range(1, count)
+    }
+    for d in reversed(range(1, count)):
+        out_copies[d].start()
+    recv[me] = send[me]
+
+    def along_y(t):
+        g = partner_of(at_grp, t, grp)
+        groups = [[] for _ in range(fan)]
+        for h in range(half):
+            loaded = [
+                recv[g * pen + h * fan + k].reshape(8 * tiles, 128) for k in range(fan)
+            ]
+            for k, tile in enumerate(regroup(loaded, block_y)):
+                groups[k].append(tile)
+        for k in range(fan):
+            rows = jnp.concatenate(groups[k], axis=1)
+            out = dot3(split(rows), cas, 1, 0)
+            start = pl.multiple_of((g * fan + k) * 8 * tiles, 128)
+            for h in range(2):
+                work[pl.ds(start + h * 8 * KX, 8 * tiles), :] = out[:, 128 * h : 128 * h + 128]
+
+    for t in range(grp):
+        for e in range(pen):
+            if t * pen + e:
+                out_copies[t * pen + e].wait_recv()
+        along_y(t)
+
+    scale = 1.0 / (math.pi * KX * KY * KZ)
+    first = pl.multiple_of(8 * me, 8)
+    factor_z = factor_col[pl.ds(first, 8), :]
+    square_z = square_col[pl.ds(first, 8), :]
+    pick = lax.broadcasted_iota(jnp.int32, (8, 1), 0)
+
+    def along_x(f, total):
+        fz = jnp.sum(jnp.where(pick == f, factor_z, 0.0), axis=0, keepdims=True) * scale
+        sz = jnp.sum(jnp.where(pick == f, square_z, 0.0), axis=0, keepdims=True)
+        rows = jnp.concatenate(
+            [work[pl.ds(f + h * 8 * KX, KX, stride=8), :] for h in range(2)], axis=1
+        )
+        spectrum = dot3((into_hi[...], into_lo[...]), split(rows), 1, 0)
+        square = square_col[...] + (square_row[...] + sz)
+        safe = jnp.where(square > 0, square, 1.0)
+        kernel = factor_col[...] * (factor_row[...] * fz) / safe
+        kernel = jnp.where(square > 0, kernel, 0.0)
+        scaled = kernel * spectrum
+        total = total + jnp.sum(scaled * spectrum, axis=0, keepdims=True)
+        out = dot3((back_hi[...], back_lo[...]), split(scaled), 1, 0)
+        for h in range(2):
+            work[pl.ds(f + h * 8 * KX, KX, stride=8), :] = out[:, 128 * h : 128 * h + 128]
+        return total
+
+    total = lax.fori_loop(0, 8, along_x, jnp.zeros((1, KY), jnp.float32))
+    part[...] = jnp.broadcast_to(0.5 * jnp.sum(total, axis=1, keepdims=True), (1, 128))
+    sums[me] = part[...]
+
+    back_copies = {
+        d: copy_of(d, lambda p: send_back.at[p], recv_back, (back_send_sem, back_recv_sem))
+        for d in range(1, count)
+    }
+    sum_copies = {
+        d: copy_of(d, lambda p: part, sums, (sum_send_sem, sum_recv_sem))
+        for d in range(1, count)
+    }
+    for t in reversed(range(grp)):
+        g = partner_of(at_grp, t, grp)
+        groups = [[] for _ in range(half)]
+        for k in range(fan):
+            start = pl.multiple_of((g * fan + k) * 8 * tiles, 128)
+            rows = jnp.concatenate(
+                [work[pl.ds(start + h * 8 * KX, 8 * tiles), :] for h in range(2)], axis=1
+            )
+            out = dot3(split(rows), cas, 1, 0)
+            for h in range(half):
+                groups[h].append(out[:, 128 * h : 128 * h + 128])
+        for h in range(half):
+            for k, tile in enumerate(regroup(groups[h], block_y)):
+                send_back[g * pen + h * fan + k] = tile.reshape(tiles, 8, 128)
+        for e in reversed(range(pen)):
+            if t * pen + e:
+                back_copies[t * pen + e].start()
+    for d in range(1, count):
+        sum_copies[d].start()
+    recv_back[me] = send_back[me]
+    for d in range(1, count):
+        back_copies[d].wait_recv()
+
+    def home_z(i, carry):
+        rows = jnp.concatenate(
+            [recv_back[:, 2 * i + t].reshape(KZ, 128) for t in range(2)], axis=1
+        )
+        out = dot3(split(jnp.transpose(rows)), cas, 1, 0)
+        pot_ref[pl.ds(2 * fan * i, 2 * fan)] = out.reshape(2 * fan, block_y, KZ)
+        return carry
+
+    lax.fori_loop(0, tiles // 2, home_z, 0)
+    for d in range(1, count):
+        sum_copies[d].wait_recv()
+    energy_ref[...] = jnp.sum(sums[...], axis=0)
+    for d in range(1, count):
+        out_copies[d].wait_send()
+        back_copies[d].wait_send()
+        sum_copies[d].wait_send()
+
+
+def slab_potential(grid, grp, pen):
+    count = grp * pen
+    block_x, block_y = grid.shape[0], grid.shape[1]
+    fan = 128 // block_y
+    tiles = block_x // fan
+    cas = cas_table(KZ)
+    order = np.arange(KX).reshape(grp, tiles, fan).transpose(0, 2, 1).reshape(KX)
+    factor, square = spline_factor(KX)
+    tables = [*halves(cas), *halves(cas[:, order]), *halves(cas[order, :])]
+    tables += [factor[None, :], factor[:, None], square[None, :], square[:, None]]
+    tables = [jnp.asarray(table) for table in tables]
+    vmem = pl.BlockSpec(memory_space=pltpu.VMEM)
+    blocks = pltpu.VMEM((count, tiles, 8, 128), jnp.float32)
+    potential, energy = pl.pallas_call(
+        functools.partial(slab_kernel, grp, pen),
+        out_shape=[
+            jax.ShapeDtypeStruct(grid.shape, jnp.float32),
+            jax.ShapeDtypeStruct((1, 128), jnp.float32),
+        ],
+        in_specs=[vmem] * (1 + len(tables)),
+        out_specs=[vmem] * 2,
+        scratch_shapes=[
+            blocks, blocks, blocks, blocks,
+            pltpu.VMEM((16 * KX, 128), jnp.float32),
+            pltpu.VMEM((count, 1, 128), jnp.float32),
+            pltpu.VMEM((1, 128), jnp.float32),
+        ] + [pltpu.SemaphoreType.DMA((count,))] * 6,
+        compiler_params=pltpu.CompilerParams(
+            collective_id=1, has_side_effects=True, vmem_limit_bytes=60 * 1024 * 1024
+        ),
+        name="slab",
+    )(grid, *tables)
+    return (potential, energy[0, 0])
+
+
+def slab_fits(grp, pen, block_x, block_y):
+    fan = 128 // block_y
+    return (
+        grp * pen * 8 == KZ and KX == KY and KY == KZ and pen % fan == 0
+        and block_x % (2 * fan) == 0 and KZ == 256
+    )
+
+
 def local(cell_offsets, cell_z, frac, charges, tile_counts):
     block_x = KX // lax.axis_size("grp")
     block_y = KY // lax.axis_size("pen")
@@ -431,7 +676,11 @@
     merged = padded[: block_x + 5, :block_y].at[:, :5].add(rim_y)
     rim_x = shifted(merged[block_x : block_x + 5], "grp", 1)
     grid = merged[:block_x] + jnp.pad(rim_x, ((0, block_x - 5), (0, 0), (0, 0)))
-    potential, total = spectrum_of(grid, block_x, block_y)
+    grp, pen = lax.axis_size("grp"), lax.axis_size("pen")
+    if slab_fits(grp, pen, block_x, block_y):
+        potential, total = slab_potential(grid, grp, pen)
+    else:
+        potential, total = spectrum_of(grid, block_x, block_y)
     upper = shifted(potential[:5], "grp", -1)
     ext_x = jnp.concatenate([potential[:, :5], upper[:, :5]], axis=0)
     beside = shifted(ext_x, "pen", -1)

time: 400 us -> 243 us (0.61)
  local copies, waits for them, and re-layouts: 94.3 us -> 21 us
  Pallas kernels: 248 us -> 193 us
  matrix products: 18.9 us -> 0 us
  other arithmetic: 13 us -> 3.42 us
    reshape x11 -> x0, local copies, waits for them, and re-layouts: 55.7 us -> none  [the longest x2 11.5 us: spectrum_of(): columns.reshape(pen, 2, block_y, planes, block_x).transpose(0, 1, 3, 4, 2)]
    pallas_call x4 -> x1, Pallas kernels: 164 us -> 109 us  [slab_potential(): pl.pallas_call(functools.partial(slab_kernel, grp, pen), out_shape=[jax.S...]
    dot_general x6 -> x0, matrix products: 18.9 us -> none  [dot(): lax.dot_general(left, right, dims, precision=highest, preferred_element_t...]
    transpose x1 -> x0, local copies, waits for them, and re-layouts: 6.89 us -> none  [spectrum_of(): lines_z.reshape(pen, 2, planes, block_x, block_y).transpose(0, 1, 4, 2, 3)]
    slice x3 -> x0, local copies, waits for them, and re-layouts: 5.38 us -> none  [the longest x1 3.52 us: spectrum_of(): full = jnp.concatenate([whole, rows[..., lines:], midway], axis=-1)]
    reduce_sum x3 -> x0, other arithmetic: 4.58 us -> none  [the longest x2 2.7 us: spectrum_of(): spectral = jnp.sum(sums[:, 0, 0])]
where the time goes in v1:
time: 243 us; the launch traced here: 242 us
  Pallas kernels  193 us (79%)
  local copies, waits for them, and re-layouts  21 us (9%)
  waiting for transfers between devices  15 us (6%)
  starting transfers between devices  8.1 us (3%)
  other arithmetic  3.42 us (1%)
    pallas_call x1, Pallas kernels, slab_potential(): pl.pallas_call(functools.partial(slab_kernel, grp, pen), out_shape=[jax.S...  109 us
    pallas_call x1, Pallas kernels, local(): pl.pallas_call(functools.partial(interp_kernel, per_row, slots), out_shap...  50.6 us
    pallas_call x1, Pallas kernels, local(): pl.pallas_call(functools.partial(spread_kernel, per_row, slots), out_shap...  33.1 us
    ppermute x4, waiting for transfers between devices, shifted(): return lax.ppermute(block, axis, route)  15 us
    ppermute x4, starting transfers between devices, shifted(): return lax.ppermute(block, axis, route)  8.1 us
    scatter-add x1, local copies, waits for them, and re-layouts, local(): merged = padded[:block_x + 5, :block_y].at[:, :5].add(rim_y)  5.67 us
    unnamed x7, local copies, waits for them, and re-layouts  5.61 us
  transfers between devices with their start and end apart: 4, of which 4 were waited for; matrix products, arithmetic and copies ran while one was open for 1% of the time, Pallas kernels for 0%

profile of v1, /device:TPU:1, one launch (start us, length us, event | category | flops | bytes accessed | tf_op | source)
XLA Modules:
  0.0 242.5 jit_solution(130935354278189163)
XLA Ops:
  1.7 1.6 reshape.61.z_ref
  3.3 0.9 reshape.63
  4.3 1.7 copy.32
  5.9 1.9 copy.31
  8.5 33.1 %spread.1 = f32[72,40,256]{2,1,0:T(8,128)} custom-call(s32[2,128,256]{2,1,0:T(8,128)} %bitcast.15, s32[128,256]{1,0:T(8,128)} %reshape.61.z_ref, f32[3,128,256]{2,1,0:T(8,128)} %bitcast.13, f32[128,256]{1,0:T(8,128)} %compare_select_fusion.q_ref), custom_call_target="tpu_custom_call" | custom-call | tf_op jit(solution)/shard_map/spread/pallas_call | solution.py:667
  41.6 1.1 slice.60
  42.8 2.6 %collective-permute-start = (f32[69,5,256]{2,0,1:T(8,128)S(1)}, f32[69,5,256]{2,0,1:T(8,128)S(1)}, u32[]{:S(2)}, u32[]{:S(2)}) collective-permute-start(f32[69,5,256]{2,0,1:T(8,128)S(1)} %copy.21), channel_id=1, source_target_pairs={{7,0},{0,1},{1,2},{2,3},{3,4},{4,5},{5,6},{6,7},{15,8},{8,9},{9,10... | collective-permute-start | bytes 1059848 | tf_op jit(solution)/shard_map/ppermute | solution.py:25
  45.5 1.8 slice.58
  47.3 2.6 %collective-permute-done = f32[69,5,256]{2,0,1:T(8,128)S(1)} collective-permute-done((f32[69,5,256]{2,0,1:T(8,128)S(1)}, f32[69,5,256]{2,0,1:T(8,128)S(1)}, u32[]{:S(2)}, u32[]{:S(2)}) %collective-permute-start) | collective-permute-done | bytes 353312 | tf_op jit(solution)/shard_map/ppermute | solution.py:25
  49.9 1.2 slice_add_fusion.1
  51.2 5.7 %scatter-add.4 = f32[69,32,256]{2,1,0:T(8,128)S(1)} dynamic-update-slice(f32[69,32,256]{2,1,0:T(8,128)S(1)} %slice.58, f32[69,5,256]{2,1,0:T(8,128)S(1)} %slice_add_fusion.1, s32[]{:T(128)} %constant.53.clone.1, s32[]{:T(128)} %constant.53.clone.1, s32[]{:T(128)} %constant.53.clone.1) | dynamic-update-slice | bytes 706564 | tf_op jit(solution)/shard_map/scatter-add | solution.py:676
  56.9 1.3 collective-permute-start.1
  58.2 4.7 %collective-permute-done.1 = f32[5,32,256]{2,1,0:T(8,128)S(1)} collective-permute-done((f32[5,32,256]{2,1,0:T(8,128)S(1)}, f32[5,32,256]{2,1,0:T(8,128)S(1)}, u32[]{:S(2)}, u32[]{:S(2)}) %collective-permute-start.1) | collective-permute-done | bytes 163872 | tf_op jit(solution)/shard_map/ppermute | solution.py:25
  62.9 1.5 slice_add_fusion.grid_ref
  64.4 109.3 %slab.1 = (f32[64,32,256]{2,1,0:T(8,128)}, f32[1,128]{1,0:T(1,128)}) custom-call(f32[64,32,256]{2,1,0:T(8,128)} %slice_add_fusion.grid_ref, bf16[256,256]{1,0:T(8,128)(2,1)} %constant.55.clone.cas_hi, bf16[256,256]{1,0:T(8,128)(2,1)} %constant.56.clone.cas_lo, bf16[256,256]{1,0:T(8,128)(2,1)} %constant.57.clone.into_hi, ...), custom_call_target="tpu_custom_call" | custom-call | tf_op jit(solution)/shard_map/slab/pallas_call | solution.py:622
  173.7 0.9 slice.54
  174.6 1.9 collective-permute-start.2
  176.5 1.1 slice.55
  177.6 1.7 collective-permute-done.2.up_ref
  179.5 2.2 collective-permute-start.3
  181.8 5.9 %collective-permute-done.3 = f32[69,5,256]{2,0,1:T(8,128)S(1)} collective-permute-done((f32[69,5,256]{2,0,1:T(8,128)S(1)}, f32[69,5,256]{2,0,1:T(8,128)S(1)}, u32[]{:S(2)}, u32[]{:S(2)}) %collective-permute-start.3) | collective-permute-done | bytes 353312 | tf_op jit(solution)/shard_map/ppermute | solution.py:25
  187.8 0.9 pad.11.side_ref
  188.7 50.6 %interp.1 = f32[3,128,256]{2,1,0:T(8,128)} custom-call(s32[2,128,256]{2,1,0:T(8,128)} %bitcast.16, s32[128,256]{1,0:T(8,128)} %reshape.61.z_ref, f32[3,128,256]{2,1,0:T(8,128)} %bitcast.14, f32[128,256]{1,0:T(8,128)} %compare_select_fusion.q_ref, f32[64,32,256]{2,1,0:T(8,128)} %get-tuple-element.16.pot_ref, f32[5,32,256]{2,1,0:T(8,128)} %copy-done, ...), custom_call_target="tpu_custom_call" | custom-call | tf_op jit(solution)/shard_map/interp/pallas_call | solution.py:688
  239.3 2.1 copy.27
  (17 shorter events, 2.2 us)
Async XLA Ops:
  42.8 7.1 %collective-permute-start = (f32[69,5,256]{2,0,1:T(8,128)S(1)}, f32[69,5,256]{2,0,1:T(8,128)S(1)}, u32[]{:S(2)}, u32[]{:S(2)}) collective-permute-start(f32[69,5,256]{2,0,1:T(8,128)S(1)} %copy.21), channel_id=1, source_target_pairs={{7,0},{0,1},{1,2},{2,3},{3,4},{4,5},{5,6},{6,7},{15,8},{8,9},{9,10... | collective-permute-start | bytes 1059848 | tf_op jit(solution)/shard_map/ppermute | solution.py:25
  56.9 6.1 %collective-permute-start.1 = (f32[5,32,256]{2,1,0:T(8,128)S(1)}, f32[5,32,256]{2,1,0:T(8,128)S(1)}, u32[]{:S(2)}, u32[]{:S(2)}) collective-permute-start(f32[5,32,256]{2,1,0:T(8,128)S(1)} %slice.62), channel_id=1, source_target_pairs={{24,0},{0,8},{8,16},{16,24},{25,1},{1,9},{9,17},{17,25},{26,2},{2,... | collective-permute-start | bytes 491528 | tf_op jit(solution)/shard_map/ppermute | solution.py:25
  173.7 8.0 %copy-start.1 = (f32[1,128]{1,0:T(1,128)S(1)}, f32[1,128]{1,0:T(1,128)}, u32[]{:S(2)}) copy-start(f32[1,128]{1,0:T(1,128)} %get-tuple-element.17) | copy-start | bytes 1540
  174.6 4.7 %collective-permute-start.2 = (f32[5,32,256]{2,1,0:T(8,128)S(1)}, f32[5,32,256]{2,1,0:T(8,128)S(1)}, u32[]{:S(2)}, u32[]{:S(2)}) collective-permute-start(f32[5,32,256]{2,1,0:T(8,128)S(1)} %slice.54), channel_id=1, source_target_pairs={{8,0},{16,8},{24,16},{0,24},{9,1},{17,9},{25,17},{1,25},{10,2},{18... | collective-permute-start | bytes 491528 | tf_op jit(solution)/shard_map/ppermute | solution.py:25
  179.3 9.3 %copy-start = (f32[5,32,256]{2,1,0:T(8,128)}, f32[5,32,256]{2,1,0:T(8,128)S(1)}, u32[]{:S(2)}) copy-start(f32[5,32,256]{2,1,0:T(8,128)S(1)} %collective-permute-done.2.up_ref) | copy-start | bytes 491524
  179.5 8.2 %collective-permute-start.3 = (f32[69,5,256]{2,0,1:T(8,128)S(1)}, f32[69,5,256]{2,0,1:T(8,128)S(1)}, u32[]{:S(2)}, u32[]{:S(2)}) collective-permute-start(f32[69,5,256]{2,0,1:T(8,128)S(1)} %copy.23), channel_id=1, source_target_pairs={{1,0},{2,1},{3,2},{4,3},{5,4},{6,5},{7,6},{0,7},{9,8},{10,9},{11,1... | collective-permute-start | bytes 1059848 | tf_op jit(solution)/shard_map/ppermute | solution.py:25

commit v2 on v1

--- a/solution.py
+++ b/solution.py
@@ -51,88 +51,171 @@
     return (values, slopes)
 
 
-def select_rows(distance, values):
-    total = jnp.zeros(distance.shape, jnp.float32)
-    for j in range(6):
-        total = jnp.where(distance == j, values[j], total)
-    return total
-
-
-def select_pair(distance, values, grades):
-    total = jnp.zeros(distance.shape, jnp.float32)
-    slope = jnp.zeros(distance.shape, jnp.float32)
-    for j in range(6):
-        hit = distance == j
-        total = jnp.where(hit, values[j], total)
-        slope = jnp.where(hit, grades[j], slope)
-    return (total, slope)
-
-
 def split(values):
     high = values.astype(jnp.bfloat16)
     low = (values - high.astype(jnp.float32)).astype(jnp.bfloat16)
     return (high, low)
 
 
-def product(high, low, other, dims):
-    other_high, other_low = split(other)
-    rows = high.shape[0]
-    both = lax.dot_general(
-        jnp.concatenate([high, low], axis=0), other_high, dims, preferred_element_type=jnp.float32
-    )
-    rest = lax.dot_general(high, other_low, dims, preferred_element_type=jnp.float32)
-    return both[:rows] + both[rows:] + rest
-
-
-def row_of(values, i):
-    return [value[i : i + 1] for value in values]
-
-
-def y_offset(offset, slots):
-    lane = lax.broadcasted_iota(jnp.int32, offset.shape, 1)
-    return offset + 2 * (lane // slots)
-
-
-def spread_kernel(per_row, slots, off_ref, z_ref, frac_ref, q_ref, grid_ref):
-    width = z_ref.shape[1]
-    size_z = grid_ref.shape[2]
+def shift_rows(values, offset):
+    none = jnp.zeros_like(values[0])
+    return [
+        jnp.where(offset == 0, first, second)
+        for first, second in zip(values + [none], [none] + values)
+    ]
+
+
+def store_weights(outer, slots, off_ref, frac_ref, charge, x_ref, y_ref, z_ref, which):
+    groups, width = off_ref.shape[1], off_ref.shape[2]
+    rows = pl.ds(pl.multiple_of(outer * 8, 8), 8)
+    lane_tile = lax.broadcasted_iota(jnp.int32, (8, width), 1) // slots
+    along_x = spline_rows(frac_ref[0, rows, :])[which]
+    along_y = spline_rows(frac_ref[1, rows, :])[which]
+    along_z = spline_rows(frac_ref[2, rows, :])[which]
+    if charge is not None:
+        along_x = [value * charge for value in along_x]
+    for k, value in enumerate(shift_rows(along_x, off_ref[0, rows, :])):
+        x_ref[k, rows, :] = value
+    for k, value in enumerate(along_z):
+        z_ref[k, rows, :] = value
+    near = shift_rows(along_y, off_ref[1, rows, :])
+    none = jnp.zeros_like(near[0])
+    for r in range(16):
+        value = none
+        for tile in range(4):
+            if 0 <= r - 2 * tile < 7:
+                value = jnp.where(lane_tile == tile, near[r - 2 * tile], value)
+        for h in range(width // 128):
+            start = (h * groups + outer * 8) * 16 + r
+            y_ref[pl.ds(start, 8, stride=16), :] = value[:, 128 * h : 128 * h + 128]
+
+
+def rows_of_y(y_ref, group, groups, width):
+    parts = []
+    for h in range(width // 128):
+        start = pl.multiple_of((h * groups + group) * 16, 16)
+        parts.append(y_ref[pl.ds(start, 16), :])
+    return jnp.concatenate(parts, axis=1)
+
+
+def z_window(base, values):
+    fine = lax.broadcasted_iota(jnp.int32, (32, base.shape[1]), 0) - (base & 15)
+    total = jnp.zeros(fine.shape, jnp.float32)
+    for j in range(6):
+        total = jnp.where(fine == j, values[j], total)
+    return split(total)
+
+
+def z_masks(base):
+    coarse = jnp.broadcast_to(base // 16, (16, base.shape[1])).astype(jnp.int16)
+    return [coarse == jnp.int16(k) for k in range(16)]
+
+
+def z_weights(masks, window):
+    halves_of = []
+    for part in window:
+        lower, upper = part[:16], part[16:]
+        none = jnp.zeros_like(lower)
+        blocks = []
+        for k in range(16):
+            block = jnp.where(masks[k - 1], upper, none)
+            blocks.append(jnp.where(masks[k], lower, block))
+        halves_of.append(jnp.concatenate(blocks, axis=0))
+    return halves_of
+
+
+def dot3(left, right, left_dim, right_dim):
+    dims = (((left_dim,), (right_dim,)), ((), ()))
+    one = functools.partial(
+        lax.dot_general, dimension_numbers=dims, preferred_element_type=jnp.float32
+    )
+    return one(left[0], right[0]) + one(left[0], right[1]) + one(left[1], right[0])
+
+
+def spread_row(a, per_row, cell_ref, x_ref, y_ref, z_ref, grid_ref):
+    groups, width = cell_ref.shape
+    outs = []
+    for b in range(per_row):
+        group = a * per_row + b
+        base = cell_ref[pl.ds(group, 1), :]
+        values = [z_ref[j, pl.ds(group, 1), :] for j in range(6)]
+        weights = z_weights(z_masks(base), z_window(base, values))
+        along_y = rows_of_y(y_ref, group, groups, width)
+        pair = [x_ref[k, pl.ds(group, 1), :] * along_y for k in range(7)]
+        outs.append(dot3(split(jnp.concatenate(pair, axis=0)), weights, 1, 1))
+    for k in range(7):
+        for t in range(per_row + 1):
+            value = 0.0
+            if t < per_row:
+                value = outs[t][16 * k : 16 * k + 8]
+            if t >= 1:
+                value = value + outs[t - 1][16 * k + 8 : 16 * k + 16]
+            grid_ref[2 * a + k, 8 * t : 8 * t + 8, :] += value
+
+
+def interp_row(a, per_row, cell_ref, q_ref, plain, slope, ext_ref, out_ref):
+    groups, width = cell_ref.shape
+    for b in range(per_row):
+        group = a * per_row + b
+        row = pl.ds(group, 1)
+        base = cell_ref[row, :]
+        masks = z_masks(base)
+        footing = jnp.concatenate(
+            [ext_ref[2 * a + k, 8 * b : 8 * b + 16, :] for k in range(7)], axis=0
+        )
+        footing = split(footing)
+        both = []
+        for refs in (plain, slope):
+            window = z_window(base, [refs[2][j, row, :] for j in range(6)])
+            both.append(dot3(footing, z_weights(masks, window), 1, 0))
+        main, tilt = both
+        along_x = 0.0
+        along_y = 0.0
+        along_z = 0.0
+        for k in range(7):
+            weight, grade = plain[0][k, row, :], slope[0][k, row, :]
+            piece = main[16 * k : 16 * k + 16]
+            along_x = along_x + grade * piece
+            along_y = along_y + weight * piece
+            along_z = along_z + weight * tilt[16 * k : 16 * k + 16]
+        weight_y = rows_of_y(plain[1], group, groups, width)
+        grade_y = rows_of_y(slope[1], group, groups, width)
+        minus_q = -q_ref[row, :]
+        pieces = (along_x * weight_y, along_y * grade_y, along_z * weight_y)
+        for d, piece in enumerate(pieces):
+            out_ref[d, row, :] = minus_q * jnp.sum(piece, axis=0, keepdims=True)
+
+
+def weight_scratch(groups, width):
+    return [
+        pltpu.VMEM((7, groups, width), jnp.float32),
+        pltpu.VMEM((groups * 16 * (width // 128), 128), jnp.float32),
+        pltpu.VMEM((6, groups, width), jnp.float32),
+    ]
+
+
+def spread_kernel(per_row, slots, off_ref, z_ref, frac_ref, q_ref, grid_ref, *weights):
     grid_ref[...] = jnp.zeros_like(grid_ref)
-
-    def step(outer, carry):
+    groups = z_ref.shape[0]
+
+    def prepare(outer, carry):
         rows = pl.ds(pl.multiple_of(outer * 8, 8), 8)
-        theta_x, _ = spline_rows(frac_ref[0, rows, :])
-        theta_y, _ = spline_rows(frac_ref[1, rows, :])
-        theta_z, _ = spline_rows(frac_ref[2, rows, :])
-        charge = q_ref[rows, :]
-        theta_x = [theta * charge for theta in theta_x]
-        off_x = off_ref[0, rows, :]
-        off_y = y_offset(off_ref[1, rows, :], slots)
-        base = z_ref[rows, :]
-        eight = lax.broadcasted_iota(jnp.int32, (8, width), 0)
-        sixteen = lax.broadcasted_iota(jnp.int32, (16, width), 0)
-        cells = lax.broadcasted_iota(jnp.int32, (size_z, width), 0)
-        for i in range(8):
-            weight_x = select_rows(eight - off_x[i : i + 1], row_of(theta_x, i))
-            weight_y = select_rows(sixteen - off_y[i : i + 1], row_of(theta_y, i))
-            weight_z = select_rows(
-                (cells - base[i : i + 1]) & (size_z - 1), row_of(theta_z, i)
-            )
-            pair = jnp.concatenate([weight_x[k : k + 1] * weight_y for k in range(8)], axis=0)
-            high, low = split(pair)
-            out = product(high, low, weight_z, (((1,), (1,)), ((), ())))
-            first = 2 * (outer * (8 // per_row) + i // per_row)
-            y0 = 8 * (i % per_row)
-            for k in range(8):
-                grid_ref[first + k, y0 : y0 + 16, :] += out[16 * k : 16 * k + 16]
+        store_weights(outer, slots, off_ref, frac_ref, q_ref[rows, :], *weights, 0)
         return carry
 
-    lax.fori_loop(0, z_ref.shape[0] // 8, step, 0)
+    def step(a, carry):
+        spread_row(a, per_row, z_ref, *weights, grid_ref)
+        return carry
+
+    lax.fori_loop(0, groups // 8, prepare, 0)
+    lax.fori_loop(0, groups // per_row, step, 0)
 
 
 def interp_kernel(
-    per_row, slots, off_ref, z_ref, frac_ref, q_ref, pot_ref, up_ref, side_ref, out_ref, ext_ref
+    per_row, slots, off_ref, z_ref, frac_ref, q_ref, pot_ref, up_ref, side_ref, out_ref,
+    ext_ref, *weights
 ):
-    width = z_ref.shape[1]
+    groups = z_ref.shape[0]
     size_z = pot_ref.shape[2]
     block_x, block_y = pot_ref.shape[0], pot_ref.shape[1]
     ext_ref[:block_x, :block_y] = pot_ref[...]
@@ -141,54 +224,17 @@
     ext_ref[: block_x + 5, block_y:] = side_ref[...]
     ext_ref[block_x + 5 :, block_y:] = jnp.zeros((3, 8, size_z), jnp.float32)
 
-    def step(outer, carry):
-        rows = pl.ds(pl.multiple_of(outer * 8, 8), 8)
-        theta_x, slope_x = spline_rows(frac_ref[0, rows, :])
-        theta_y, slope_y = spline_rows(frac_ref[1, rows, :])
-        theta_z, slope_z = spline_rows(frac_ref[2, rows, :])
-        off_x = off_ref[0, rows, :]
-        off_y = y_offset(off_ref[1, rows, :], slots)
-        base = z_ref[rows, :]
-        eight = lax.broadcasted_iota(jnp.int32, (8, width), 0)
-        sixteen = lax.broadcasted_iota(jnp.int32, (16, width), 0)
-        cells = lax.broadcasted_iota(jnp.int32, (size_z, width), 0)
-        dims = (((1,), (0,)), ((), ()))
-        forces = [[], [], []]
-        for i in range(8):
-            weight_x, grade_x = select_pair(
-                eight - off_x[i : i + 1], row_of(theta_x, i), row_of(slope_x, i)
-            )
-            weight_y, grade_y = select_pair(
-                sixteen - off_y[i : i + 1], row_of(theta_y, i), row_of(slope_y, i)
-            )
-            weight_z, grade_z = select_pair(
-                (cells - base[i : i + 1]) & (size_z - 1), row_of(theta_z, i), row_of(slope_z, i)
-            )
-            first = 2 * (outer * (8 // per_row) + i // per_row)
-            y0 = 8 * (i % per_row)
-            footing = jnp.concatenate(
-                [ext_ref[first + k, y0 : y0 + 16, :] for k in range(8)], axis=0
-            )
-            high, low = split(footing)
-            main = product(high, low, weight_z, dims)
-            tilt = product(high, low, grade_z, dims)
-            along_x = 0.0
-            along_y = 0.0
-            along_z = 0.0
-            for k in range(8):
-                piece = main[16 * k : 16 * k + 16]
-                along_x = along_x + grade_x[k : k + 1] * piece
-                along_y = along_y + weight_x[k : k + 1] * piece
-                along_z = along_z + weight_x[k : k + 1] * tilt[16 * k : 16 * k + 16]
-            forces[0].append(jnp.sum(along_x * weight_y, axis=0, keepdims=True))
-            forces[1].append(jnp.sum(along_y * grade_y, axis=0, keepdims=True))
-            forces[2].append(jnp.sum(along_z * weight_y, axis=0, keepdims=True))
-        minus_q = -q_ref[rows, :]
-        for d in range(3):
-            out_ref[d, rows, :] = minus_q * jnp.concatenate(forces[d], axis=0)
+    def prepare(outer, carry):
+        store_weights(outer, slots, off_ref, frac_ref, None, *weights[:3], 0)
+        store_weights(outer, slots, off_ref, frac_ref, None, *weights[3:], 1)
         return carry
 
-    lax.fori_loop(0, z_ref.shape[0] // 8, step, 0)
+    def step(a, carry):
+        interp_row(a, per_row, z_ref, q_ref, weights[:3], weights[3:], ext_ref, out_ref)
+        return carry
+
+    lax.fori_loop(0, groups // 8, prepare, 0)
+    lax.fori_loop(0, groups // per_row, step, 0)
 
 
 def modulus(index, length):
@@ -427,14 +473,6 @@
     return (factor.astype(np.float32), square.astype(np.float32))
 
 
-def dot3(left, right, left_dim, right_dim):
-    dims = (((left_dim,), (right_dim,)), ((), ()))
-    one = functools.partial(
-        lax.dot_general, dimension_numbers=dims, preferred_element_type=jnp.float32
-    )
-    return one(left[0], right[0]) + one(left[0], right[1]) + one(left[1], right[0])
-
-
 def regroup(tiles, width):
     lane = lax.broadcasted_iota(jnp.int32, tiles[0].shape, 1) // width
     bit = 1
@@ -669,6 +707,7 @@
         out_shape=jax.ShapeDtypeStruct((block_x + 8, block_y + 8, KZ), jnp.float32),
         in_specs=[vmem] * 4,
         out_specs=vmem,
+        scratch_shapes=weight_scratch(groups, width),
         compiler_params=params,
         name="spread",
     )(offsets, zcell, fracs, live_q)
@@ -690,7 +729,8 @@
         out_shape=jax.ShapeDtypeStruct((3, groups, width), jnp.float32),
         in_specs=[vmem] * 7,
         out_specs=vmem,
-        scratch_shapes=[pltpu.VMEM((block_x + 8, block_y + 8, KZ), jnp.float32)],
+        scratch_shapes=[pltpu.VMEM((block_x + 8, block_y + 8, KZ), jnp.float32)]
+        + 2 * weight_scratch(groups, width),
         compiler_params=params,
         name="interp",
     )(offsets, zcell, fracs, live_q, potential, upper, beside)

time: 243 us -> 213 us (0.88)
  Pallas kernels: 193 us -> 163 us
    pallas_call x1, Pallas kernels: 50.6 us -> 27.6 us  [local(): pl.pallas_call(functools.partial(interp_kernel, per_row, slots), out_shap...]
    pallas_call x1, Pallas kernels: 33.1 us -> 26.6 us  [local(): pl.pallas_call(functools.partial(spread_kernel, per_row, slots), out_shap...]
where the time goes in v2:
time: 213 us
  Pallas kernels  163 us (77%)
  local copies, waits for them, and re-layouts  21 us (10%)
  waiting for transfers between devices  15 us (7%)
  starting transfers between devices  7.92 us (4%)
  other arithmetic  3.42 us (2%)
    pallas_call x1, Pallas kernels, slab_potential(): pl.pallas_call(functools.partial(slab_kernel, grp, pen), out_shape=[jax.S...  109 us
    pallas_call x1, Pallas kernels, local(): pl.pallas_call(functools.partial(interp_kernel, per_row, slots), out_shap...  27.6 us
    pallas_call x1, Pallas kernels, local(): pl.pallas_call(functools.partial(spread_kernel, per_row, slots), out_shap...  26.6 us
    ppermute x4, waiting for transfers between devices, shifted(): return lax.ppermute(block, axis, route)  15 us
    ppermute x4, starting transfers between devices, shifted(): return lax.ppermute(block, axis, route)  7.92 us
    scatter-add x1, local copies, waits for them, and re-layouts, local(): merged = padded[:block_x + 5, :block_y].at[:, :5].add(rim_y)  5.67 us
    unnamed x7, local copies, waits for them, and re-layouts  5.61 us
  transfers between devices with their start and end apart: 4, of which 4 were waited for; matrix products, arithmetic and copies ran while one was open for 1% of the time, Pallas kernels for 0%

profile of v2, /device:TPU:1, one launch (start us, length us, event | category | flops | bytes accessed | tf_op | source)
XLA Modules:
  0.0 212.8 jit_solution(9225950836101356959)
XLA Ops:
  1.7 1.6 reshape.61.z_ref
  3.3 0.9 reshape.63
  4.3 1.7 copy.32
  5.9 1.9 copy.31
  8.5 26.6 %spread.1 = f32[72,40,256]{2,1,0:T(8,128)} custom-call(s32[2,128,256]{2,1,0:T(8,128)} %bitcast.15, s32[128,256]{1,0:T(8,128)} %reshape.61.z_ref, f32[3,128,256]{2,1,0:T(8,128)} %bitcast.13, f32[128,256]{1,0:T(8,128)} %compare_select_fusion.q_ref), custom_call_target="tpu_custom_call" | custom-call | tf_op jit(solution)/shard_map/spread/pallas_call | solution.py:705
  35.1 1.1 slice.60
  36.3 2.6 %collective-permute-start = (f32[69,5,256]{2,0,1:T(8,128)S(1)}, f32[69,5,256]{2,0,1:T(8,128)S(1)}, u32[]{:S(2)}, u32[]{:S(2)}) collective-permute-start(f32[69,5,256]{2,0,1:T(8,128)S(1)} %copy.21), channel_id=1, source_target_pairs={{7,0},{0,1},{1,2},{2,3},{3,4},{4,5},{5,6},{6,7},{15,8},{8,9},{9,10... | collective-permute-start | bytes 1059848 | tf_op jit(solution)/shard_map/ppermute | solution.py:25
  38.9 1.8 slice.58
  40.8 2.6 %collective-permute-done = f32[69,5,256]{2,0,1:T(8,128)S(1)} collective-permute-done((f32[69,5,256]{2,0,1:T(8,128)S(1)}, f32[69,5,256]{2,0,1:T(8,128)S(1)}, u32[]{:S(2)}, u32[]{:S(2)}) %collective-permute-start) | collective-permute-done | bytes 353312 | tf_op jit(solution)/shard_map/ppermute | solution.py:25
  43.4 1.2 slice_add_fusion.1
  44.6 5.7 %scatter-add.4 = f32[69,32,256]{2,1,0:T(8,128)S(1)} dynamic-update-slice(f32[69,32,256]{2,1,0:T(8,128)S(1)} %slice.58, f32[69,5,256]{2,1,0:T(8,128)S(1)} %slice_add_fusion.1, s32[]{:T(128)} %constant.53.clone.1, s32[]{:T(128)} %constant.53.clone.1, s32[]{:T(128)} %constant.53.clone.1) | dynamic-update-slice | bytes 706564 | tf_op jit(solution)/shard_map/scatter-add | solution.py:715
  50.3 1.4 collective-permute-start.1
  51.7 4.7 %collective-permute-done.1 = f32[5,32,256]{2,1,0:T(8,128)S(1)} collective-permute-done((f32[5,32,256]{2,1,0:T(8,128)S(1)}, f32[5,32,256]{2,1,0:T(8,128)S(1)}, u32[]{:S(2)}, u32[]{:S(2)}) %collective-permute-start.1) | collective-permute-done | bytes 163872 | tf_op jit(solution)/shard_map/ppermute | solution.py:25
  56.4 1.5 slice_add_fusion.grid_ref
  57.9 109.2 %slab.1 = (f32[64,32,256]{2,1,0:T(8,128)}, f32[1,128]{1,0:T(1,128)}) custom-call(f32[64,32,256]{2,1,0:T(8,128)} %slice_add_fusion.grid_ref, bf16[256,256]{1,0:T(8,128)(2,1)} %constant.55.clone.cas_hi, bf16[256,256]{1,0:T(8,128)(2,1)} %constant.56.clone.cas_lo, bf16[256,256]{1,0:T(8,128)(2,1)} %constant.57.clone.into_hi, ...), custom_call_target="tpu_custom_call" | custom-call | tf_op jit(solution)/shard_map/slab/pallas_call | solution.py:660
  167.1 0.9 slice.54
  168.1 1.9 collective-permute-start.2
  170.0 1.1 slice.55
  171.1 1.7 collective-permute-done.2.up_ref
  173.0 2.0 collective-permute-start.3
  175.0 5.9 %collective-permute-done.3 = f32[69,5,256]{2,0,1:T(8,128)S(1)} collective-permute-done((f32[69,5,256]{2,0,1:T(8,128)S(1)}, f32[69,5,256]{2,0,1:T(8,128)S(1)}, u32[]{:S(2)}, u32[]{:S(2)}) %collective-permute-start.3) | collective-permute-done | bytes 353312 | tf_op jit(solution)/shard_map/ppermute | solution.py:25
  181.1 0.9 pad.11.side_ref
  181.9 27.6 %interp.1 = f32[3,128,256]{2,1,0:T(8,128)} custom-call(s32[2,128,256]{2,1,0:T(8,128)} %bitcast.16, s32[128,256]{1,0:T(8,128)} %reshape.61.z_ref, f32[3,128,256]{2,1,0:T(8,128)} %bitcast.14, f32[128,256]{1,0:T(8,128)} %compare_select_fusion.q_ref, f32[64,32,256]{2,1,0:T(8,128)} %get-tuple-element.16.pot_ref, f32[5,32,256]{2,1,0:T(8,128)} %copy-done, ...), custom_call_target="tpu_custom_call" | custom-call | tf_op jit(solution)/shard_map/interp/pallas_call | solution.py:727
  209.6 2.1 copy.27
  (17 shorter events, 2.2 us)
Async XLA Ops:
  36.3 7.1 %collective-permute-start = (f32[69,5,256]{2,0,1:T(8,128)S(1)}, f32[69,5,256]{2,0,1:T(8,128)S(1)}, u32[]{:S(2)}, u32[]{:S(2)}) collective-permute-start(f32[69,5,256]{2,0,1:T(8,128)S(1)} %copy.21), channel_id=1, source_target_pairs={{7,0},{0,1},{1,2},{2,3},{3,4},{4,5},{5,6},{6,7},{15,8},{8,9},{9,10... | collective-permute-start | bytes 1059848 | tf_op jit(solution)/shard_map/ppermute | solution.py:25
  50.3 6.1 %collective-permute-start.1 = (f32[5,32,256]{2,1,0:T(8,128)S(1)}, f32[5,32,256]{2,1,0:T(8,128)S(1)}, u32[]{:S(2)}, u32[]{:S(2)}) collective-permute-start(f32[5,32,256]{2,1,0:T(8,128)S(1)} %slice.62), channel_id=1, source_target_pairs={{24,0},{0,8},{8,16},{16,24},{25,1},{1,9},{9,17},{17,25},{26,2},{2,... | collective-permute-start | bytes 491528 | tf_op jit(solution)/shard_map/ppermute | solution.py:25
  167.1 7.9 %copy-start.1 = (f32[1,128]{1,0:T(1,128)S(1)}, f32[1,128]{1,0:T(1,128)}, u32[]{:S(2)}) copy-start(f32[1,128]{1,0:T(1,128)} %get-tuple-element.17) | copy-start | bytes 1540
  168.1 4.7 %collective-permute-start.2 = (f32[5,32,256]{2,1,0:T(8,128)S(1)}, f32[5,32,256]{2,1,0:T(8,128)S(1)}, u32[]{:S(2)}, u32[]{:S(2)}) collective-permute-start(f32[5,32,256]{2,1,0:T(8,128)S(1)} %slice.54), channel_id=1, source_target_pairs={{8,0},{16,8},{24,16},{0,24},{9,1},{17,9},{25,17},{1,25},{10,2},{18... | collective-permute-start | bytes 491528 | tf_op jit(solution)/shard_map/ppermute | solution.py:25
  172.8 9.2 %copy-start = (f32[5,32,256]{2,1,0:T(8,128)}, f32[5,32,256]{2,1,0:T(8,128)S(1)}, u32[]{:S(2)}) copy-start(f32[5,32,256]{2,1,0:T(8,128)S(1)} %collective-permute-done.2.up_ref) | copy-start | bytes 491524
  173.0 8.0 %collective-permute-start.3 = (f32[69,5,256]{2,0,1:T(8,128)S(1)}, f32[69,5,256]{2,0,1:T(8,128)S(1)}, u32[]{:S(2)}, u32[]{:S(2)}) collective-permute-start(f32[69,5,256]{2,0,1:T(8,128)S(1)} %copy.23), channel_id=1, source_target_pairs={{1,0},{2,1},{3,2},{4,3},{5,4},{6,5},{7,6},{0,7},{9,8},{10,9},{11,1... | collective-permute-start | bytes 1059848 | tf_op jit(solution)/shard_map/ppermute | solution.py:25

commit v3 on v2

--- a/solution.py
+++ b/solution.py
@@ -65,15 +65,13 @@
     ]
 
 
-def store_weights(outer, slots, off_ref, frac_ref, charge, x_ref, y_ref, z_ref, which):
+def store_weights(outer, slots, off_ref, frac_ref, x_ref, y_ref, z_ref, which):
     groups, width = off_ref.shape[1], off_ref.shape[2]
     rows = pl.ds(pl.multiple_of(outer * 8, 8), 8)
     lane_tile = lax.broadcasted_iota(jnp.int32, (8, width), 1) // slots
     along_x = spline_rows(frac_ref[0, rows, :])[which]
     along_y = spline_rows(frac_ref[1, rows, :])[which]
     along_z = spline_rows(frac_ref[2, rows, :])[which]
-    if charge is not None:
-        along_x = [value * charge for value in along_x]
     for k, value in enumerate(shift_rows(along_x, off_ref[0, rows, :])):
         x_ref[k, rows, :] = value
     for k, value in enumerate(along_z):
@@ -132,7 +130,7 @@
     return one(left[0], right[0]) + one(left[0], right[1]) + one(left[1], right[0])
 
 
-def spread_row(a, per_row, cell_ref, x_ref, y_ref, z_ref, grid_ref):
+def spread_row(a, per_row, cell_ref, q_ref, x_ref, y_ref, z_ref, grid_ref):
     groups, width = cell_ref.shape
     outs = []
     for b in range(per_row):
@@ -140,7 +138,7 @@
         base = cell_ref[pl.ds(group, 1), :]
         values = [z_ref[j, pl.ds(group, 1), :] for j in range(6)]
         weights = z_weights(z_masks(base), z_window(base, values))
-        along_y = rows_of_y(y_ref, group, groups, width)
+        along_y = rows_of_y(y_ref, group, groups, width) * q_ref[pl.ds(group, 1), :]
         pair = [x_ref[k, pl.ds(group, 1), :] * along_y for k in range(7)]
         outs.append(dot3(split(jnp.concatenate(pair, axis=0)), weights, 1, 1))
     for k in range(7):
@@ -199,12 +197,11 @@
     groups = z_ref.shape[0]
 
     def prepare(outer, carry):
-        rows = pl.ds(pl.multiple_of(outer * 8, 8), 8)
-        store_weights(outer, slots, off_ref, frac_ref, q_ref[rows, :], *weights, 0)
+        store_weights(outer, slots, off_ref, frac_ref, *weights, 0)
         return carry
 
     def step(a, carry):
-        spread_row(a, per_row, z_ref, *weights, grid_ref)
+        spread_row(a, per_row, z_ref, q_ref, *weights, grid_ref)
         return carry
 
     lax.fori_loop(0, groups // 8, prepare, 0)
@@ -225,8 +222,8 @@
     ext_ref[block_x + 5 :, block_y:] = jnp.zeros((3, 8, size_z), jnp.float32)
 
     def prepare(outer, carry):
-        store_weights(outer, slots, off_ref, frac_ref, None, *weights[:3], 0)
-        store_weights(outer, slots, off_ref, frac_ref, None, *weights[3:], 1)
+        store_weights(outer, slots, off_ref, frac_ref, *weights[:3], 0)
+        store_weights(outer, slots, off_ref, frac_ref, *weights[3:], 1)
         return carry
 
     def step(a, carry):
@@ -491,81 +488,210 @@
     return tiles
 
 
-def slab_kernel(
-    grp, pen, grid_ref, cas_hi, cas_lo, into_hi, into_lo, back_hi, back_lo,
-    factor_row, factor_col, square_row, square_col, pot_ref, energy_ref,
+def whole_kernel(
+    grp, pen, slots, off_ref, cell_ref, frac_ref, q_ref, cas_hi, cas_lo, into_hi, into_lo,
+    back_hi, back_lo, factor_row, factor_col, square_row, square_col, out_ref, energy_ref,
+    pad, ext, plain_x, plain_y, plain_z, slope_x, slope_y, slope_z,
     send, recv, send_back, recv_back, work, sums, part,
-    send_sem, recv_sem, back_send_sem, back_recv_sem, sum_send_sem, sum_recv_sem,
+    rim_side, rim_up, rim_corner, halo_side, halo_up, halo_corner,
+    out_send, out_recv, back_send, back_recv, sum_send, sum_recv,
+    side_send, side_recv, halo_send, halo_recv, edge_send, edge_recv,
 ):
     count = grp * pen
-    block_x, block_y = grid_ref.shape[0], grid_ref.shape[1]
+    slabs, blocks = send.shape[0], send.shape[2]
+    groups = cell_ref.shape[0]
+    block_x, block_y = KX // grp, KY // pen
+    tile_rows = block_x // 2
+    per_row = groups // tile_rows
     fan = 128 // block_y
-    tiles = block_x // fan
+    depth = block_x // slabs
+    step = depth // 2
     half = pen // fan
+    lines = 8 * blocks
     at_grp, at_pen = lax.axis_index("grp"), lax.axis_index("pen")
     me = at_grp * pen + at_pen
+    plain = (plain_x, plain_y, plain_z)
+    slope = (slope_x, slope_y, slope_z)
+    cas = (cas_hi[...], cas_lo[...])
+
+    def device(d_grp, d_pen):
+        return {
+            "grp": lax.rem(at_grp + d_grp + grp, grp),
+            "pen": lax.rem(at_pen + d_pen + pen, pen),
+        }
+
+    def remote(source, target, sems, where):
+        return pltpu.make_async_remote_copy(
+            src_ref=source, dst_ref=target, send_sem=sems[0], recv_sem=sems[1],
+            device_id=where, device_id_type=pl.DeviceIdType.MESH,
+        )
 
     def peer_of(d):
-        peer = partner_of(me, d, count)
-        return (peer, {"grp": peer // pen, "pen": peer % pen})
+        peer = lax.rem(me + d, count)
+        return (peer, {"grp": lax.div(peer, pen), "pen": lax.rem(peer, pen)})
+
+    def fan_out(make):
+        def one(e, carry):
+            make(1 + lax.rem(e + pen - 1, count - 1)).start()
+            return carry
+
+        lax.fori_loop(0, count - 1, one, 0)
+
+    def fan_wait(make, receiving):
+        def one(d, carry):
+            copy = make(d)
+            copy.wait_recv() if receiving else copy.wait_send()
+            return carry
+
+        lax.fori_loop(1, count, one, 0)
+
+    def out_copy(s):
+        def make(d):
+            peer, where = peer_of(d)
+            sems = (out_send.at[s, d], out_recv.at[s, d])
+            return remote(send.at[s, peer], recv.at[s, me], sems, where)
+
+        return make
+
+    def back_copy(s):
+        def make(d):
+            peer, where = peer_of(d)
+            sems = (back_send.at[s, d], back_recv.at[s, d])
+            return remote(send_back.at[s, peer], recv_back.at[s, me], sems, where)
+
+        return make
+
+    def sum_copy(d):
+        return remote(part, sums.at[me], (sum_send.at[d], sum_recv.at[d]), peer_of(d)[1])
+
+    def slab_rows(s):
+        return pl.ds(s * depth, depth)
+
+    def side_rim(s):
+        source = pad.at[slab_rows(s), pl.ds(block_y, 8), :]
+        return remote(source, rim_side.at[s], (side_send.at[s], side_recv.at[s]), device(0, 1))
+
+    def edge_rims():
+        source = pad.at[pl.ds(block_x, 5)]
+        return [
+            remote(
+                source.at[:, pl.ds(0, block_y), :], rim_up,
+                (edge_send.at[0], edge_recv.at[0]), device(1, 0),
+            ),
+            remote(
+                source.at[:, pl.ds(block_y, 8), :], rim_corner,
+                (edge_send.at[1], edge_recv.at[1]), device(1, 1),
+            ),
+        ]
+
+    def side_halo(s):
+        source = ext.at[slab_rows(s), pl.ds(0, 8), :]
+        return remote(source, halo_side.at[s], (halo_send.at[s], halo_recv.at[s]), device(0, -1))
+
+    def edge_halos():
+        source = ext.at[pl.ds(0, 5)]
+        return [
+            remote(
+                source.at[:, pl.ds(0, block_y), :], halo_up,
+                (edge_send.at[2], edge_recv.at[2]), device(-1, 0),
+            ),
+            remote(
+                source.at[:, pl.ds(0, 8), :], halo_corner,
+                (edge_send.at[3], edge_recv.at[3]), device(-1, -1),
+            ),
+        ]
 
     barrier = pltpu.get_barrier_semaphore()
-    for d in range(1, count):
+
+    def greet(d, carry):
         pl.semaphore_signal(
             barrier, inc=1, device_id=peer_of(d)[1], device_id_type=pl.DeviceIdType.MESH
         )
-    cas = (cas_hi[...], cas_lo[...])
-
-    def along_z(i, carry):
-        rows = grid_ref[pl.ds(2 * fan * i, 2 * fan)].reshape(256, KZ)
-        out = dot3(cas, split(rows), 1, 1)
-        for t in range(2):
-            send[:, 2 * i + t] = out[:, 128 * t : 128 * t + 128].reshape(count, 8, 128)
-        return carry
-
-    lax.fori_loop(0, tiles // 2, along_z, 0)
+        return carry
+
+    lax.fori_loop(1, count, greet, 0)
+    pad[...] = jnp.zeros_like(pad)
+
+    def prepare(outer, carry):
+        store_weights(outer, slots, off_ref, frac_ref, *plain, 0)
+        return carry
+
+    lax.fori_loop(0, groups // 8, prepare, 0)
     pl.semaphore_wait(barrier, count - 1)
 
-    def copy_of(d, source, target, sems):
-        peer, where = peer_of(d)
-        return pltpu.make_async_remote_copy(
-            src_ref=source(peer),
-            dst_ref=target.at[me],
-            send_sem=sems[0].at[d],
-            recv_sem=sems[1].at[d],
-            device_id=where,
-            device_id_type=pl.DeviceIdType.MESH,
-        )
-
-    out_copies = {
-        d: copy_of(d, lambda p: send.at[p], recv, (send_sem, recv_sem))
-        for d in range(1, count)
-    }
-    for d in reversed(range(1, count)):
-        out_copies[d].start()
-    recv[me] = send[me]
-
-    def along_y(t):
-        g = partner_of(at_grp, t, grp)
-        groups = [[] for _ in range(fan)]
-        for h in range(half):
-            loaded = [
-                recv[g * pen + h * fan + k].reshape(8 * tiles, 128) for k in range(fan)
-            ]
-            for k, tile in enumerate(regroup(loaded, block_y)):
-                groups[k].append(tile)
-        for k in range(fan):
-            rows = jnp.concatenate(groups[k], axis=1)
-            out = dot3(split(rows), cas, 1, 0)
-            start = pl.multiple_of((g * fan + k) * 8 * tiles, 128)
-            for h in range(2):
-                work[pl.ds(start + h * 8 * KX, 8 * tiles), :] = out[:, 128 * h : 128 * h + 128]
-
-    for t in range(grp):
-        for e in range(pen):
-            if t * pen + e:
-                out_copies[t * pen + e].wait_recv()
-        along_y(t)
+    def ship(s):
+        side_rim(s).wait_recv()
+        pad[slab_rows(s), pl.ds(0, 8), :] += rim_side[s]
+
+    def transform_out(s):
+        def along_z(i, carry):
+            rows = pad[pl.ds(s * depth + 2 * fan * i, 2 * fan), pl.ds(0, block_y), :]
+            out = dot3(cas, split(rows.reshape(256, KZ)), 1, 1)
+            for t in range(2):
+                block = out[:, 128 * t : 128 * t + 128].reshape(count, 8, 128)
+                send[s, :, 2 * i + t] = block
+            return carry
+
+        lax.fori_loop(0, blocks // 2, along_z, 0)
+        fan_out(out_copy(s))
+        recv[s, me] = send[s, me]
+
+    def spread_step(i, carry):
+        a = tile_rows - 1 - i
+        spread_row(a, per_row, cell_ref, q_ref, *plain, pad)
+
+        @pl.when(((lax.rem(a + 3, step) == 0) & (a + 3 < tile_rows)) | (a == 0))
+        def _():
+            side_rim(lax.div(a + 3, step)).start()
+
+        @pl.when(a == tile_rows - step - 3)
+        def _():
+            for copy in edge_rims():
+                copy.start()
+
+        @pl.when((lax.rem(a + 7, step) == 0) & (a + 7 < tile_rows))
+        def _():
+            s = lax.div(a + 7, step)
+            ship(s)
+            transform_out(s)
+
+        return carry
+
+    lax.fori_loop(0, tile_rows, spread_step, 0)
+    for copy in edge_rims():
+        copy.wait_recv()
+    ship(0)
+    pad[:5, :block_y, :] += rim_up[...]
+    pad[:5, :8, :] += rim_corner[...]
+    transform_out(0)
+
+    def prepare_slopes(outer, carry):
+        store_weights(outer, slots, off_ref, frac_ref, *slope, 1)
+        return carry
+
+    lax.fori_loop(0, groups // 8, prepare_slopes, 0)
+
+    def along_y(i, carry):
+        s = slabs - 1 - i
+        fan_wait(out_copy(s), True)
+        rows = []
+        for g in range(grp):
+            parts = [[] for _ in range(fan)]
+            for h in range(half):
+                loaded = [
+                    recv[s, g * pen + h * fan + k].reshape(lines, 128) for k in range(fan)
+                ]
+                for k, tile in enumerate(regroup(loaded, block_y)):
+                    parts[k].append(tile)
+            rows += [jnp.concatenate(part, axis=1) for part in parts]
+        out = dot3(split(jnp.concatenate(rows, axis=0)), cas, 1, 0)
+        span = grp * fan * lines
+        for h in range(2):
+            start = pl.multiple_of(s * span + h * 8 * KX, 128)
+            work[pl.ds(start, span), :] = out[:, 128 * h : 128 * h + 128]
+        return carry
+
+    lax.fori_loop(0, slabs, along_y, 0)
 
     scale = 1.0 / (math.pi * KX * KY * KZ)
     first = pl.multiple_of(8 * me, 8)
@@ -595,95 +721,152 @@
     part[...] = jnp.broadcast_to(0.5 * jnp.sum(total, axis=1, keepdims=True), (1, 128))
     sums[me] = part[...]
 
-    back_copies = {
-        d: copy_of(d, lambda p: send_back.at[p], recv_back, (back_send_sem, back_recv_sem))
-        for d in range(1, count)
-    }
-    sum_copies = {
-        d: copy_of(d, lambda p: part, sums, (sum_send_sem, sum_recv_sem))
-        for d in range(1, count)
-    }
-    for t in reversed(range(grp)):
-        g = partner_of(at_grp, t, grp)
-        groups = [[] for _ in range(half)]
-        for k in range(fan):
-            start = pl.multiple_of((g * fan + k) * 8 * tiles, 128)
+    def back_y(s, carry):
+        span = grp * fan * lines
+        rows = jnp.concatenate(
+            [
+                work[pl.ds(pl.multiple_of(s * span + h * 8 * KX, 128), span), :]
+                for h in range(2)
+            ],
+            axis=1,
+        )
+        out = dot3(split(rows), cas, 1, 0)
+        for g in range(grp):
+            for h in range(half):
+                parts = []
+                for k in range(fan):
+                    start = (g * fan + k) * lines
+                    parts.append(out[start : start + lines, 128 * h : 128 * h + 128])
+                for k, tile in enumerate(regroup(parts, block_y)):
+                    send_back[s, g * pen + h * fan + k] = tile.reshape(blocks, 8, 128)
+        fan_out(back_copy(s))
+        recv_back[s, me] = send_back[s, me]
+        return carry
+
+    lax.fori_loop(0, slabs, back_y, 0)
+    fan_out(sum_copy)
+
+    def home(s, carry):
+        fan_wait(back_copy(s), True)
+
+        def home_z(i, inner):
             rows = jnp.concatenate(
-                [work[pl.ds(start + h * 8 * KX, 8 * tiles), :] for h in range(2)], axis=1
+                [recv_back[s, :, 2 * i + t].reshape(KZ, 128) for t in range(2)], axis=1
             )
-            out = dot3(split(rows), cas, 1, 0)
-            for h in range(half):
-                groups[h].append(out[:, 128 * h : 128 * h + 128])
-        for h in range(half):
-            for k, tile in enumerate(regroup(groups[h], block_y)):
-                send_back[g * pen + h * fan + k] = tile.reshape(tiles, 8, 128)
-        for e in reversed(range(pen)):
-            if t * pen + e:
-                back_copies[t * pen + e].start()
-    for d in range(1, count):
-        sum_copies[d].start()
-    recv_back[me] = send_back[me]
-    for d in range(1, count):
-        back_copies[d].wait_recv()
-
-    def home_z(i, carry):
-        rows = jnp.concatenate(
-            [recv_back[:, 2 * i + t].reshape(KZ, 128) for t in range(2)], axis=1
-        )
-        out = dot3(split(jnp.transpose(rows)), cas, 1, 0)
-        pot_ref[pl.ds(2 * fan * i, 2 * fan)] = out.reshape(2 * fan, block_y, KZ)
-        return carry
-
-    lax.fori_loop(0, tiles // 2, home_z, 0)
-    for d in range(1, count):
-        sum_copies[d].wait_recv()
+            out = dot3(split(jnp.transpose(rows)), cas, 1, 0)
+            where = pl.ds(s * depth + 2 * fan * i, 2 * fan)
+            ext[where, pl.ds(0, block_y), :] = out.reshape(2 * fan, block_y, KZ)
+            return inner
+
+        lax.fori_loop(0, blocks // 2, home_z, 0)
+        side_halo(s).start()
+        return carry
+
+    home(0, 0)
+    for copy in edge_halos():
+        copy.start()
+    home(1, 0)
+
+    def join_halo(s):
+        side_halo(s).wait_recv()
+        ext[slab_rows(s), pl.ds(block_y, 8), :] = halo_side[s]
+
+    join_halo(0)
+
+    def interp_step(a, carry):
+        @pl.when((lax.rem(a, step) == 0) & (a >= step) & (a < tile_rows - step))
+        def _():
+            home(lax.div(a, step) + 1, 0)
+
+        @pl.when((lax.rem(a + 3, step) == 0) & (a + 3 < tile_rows))
+        def _():
+            join_halo(lax.div(a + 3, step))
+
+        @pl.when(a == tile_rows - 3)
+        def _():
+            for copy in edge_halos():
+                copy.wait_recv()
+            ext[pl.ds(block_x, 5), pl.ds(0, block_y), :] = halo_up[...]
+            ext[pl.ds(block_x, 5), pl.ds(block_y, 8), :] = halo_corner[...]
+
+        interp_row(a, per_row, cell_ref, q_ref, plain, slope, ext, out_ref)
+        return carry
+
+    lax.fori_loop(0, tile_rows, interp_step, 0)
+    fan_wait(sum_copy, True)
     energy_ref[...] = jnp.sum(sums[...], axis=0)
-    for d in range(1, count):
-        out_copies[d].wait_send()
-        back_copies[d].wait_send()
-        sum_copies[d].wait_send()
-
-
-def slab_potential(grid, grp, pen):
+    fan_wait(sum_copy, False)
+
+    def drain(s, carry):
+        fan_wait(out_copy(s), False)
+        fan_wait(back_copy(s), False)
+        side_rim(s).wait_send()
+        side_halo(s).wait_send()
+        return carry
+
+    lax.fori_loop(0, slabs, drain, 0)
+    for copy in edge_rims() + edge_halos():
+        copy.wait_send()
+
+
+def whole_program(offsets, zcell, fracs, live_q, slots, grp, pen, slabs):
     count = grp * pen
-    block_x, block_y = grid.shape[0], grid.shape[1]
+    groups, width = zcell.shape
+    block_x, block_y = KX // grp, KY // pen
     fan = 128 // block_y
-    tiles = block_x // fan
+    blocks = block_x // fan // slabs
+    depth = block_x // slabs
     cas = cas_table(KZ)
-    order = np.arange(KX).reshape(grp, tiles, fan).transpose(0, 2, 1).reshape(KX)
+    order = np.arange(KX).reshape(grp, slabs, blocks, fan).transpose(1, 0, 3, 2).reshape(KX)
     factor, square = spline_factor(KX)
     tables = [*halves(cas), *halves(cas[:, order]), *halves(cas[order, :])]
     tables += [factor[None, :], factor[:, None], square[None, :], square[:, None]]
     tables = [jnp.asarray(table) for table in tables]
     vmem = pl.BlockSpec(memory_space=pltpu.VMEM)
-    blocks = pltpu.VMEM((count, tiles, 8, 128), jnp.float32)
-    potential, energy = pl.pallas_call(
-        functools.partial(slab_kernel, grp, pen),
+
+    def held(*shape):
+        return pltpu.VMEM(shape, jnp.float32)
+
+    traffic = held(slabs, count, blocks, 8, 128)
+    dma = pltpu.SemaphoreType.DMA
+    forces, energy = pl.pallas_call(
+        functools.partial(whole_kernel, grp, pen, slots),
         out_shape=[
-            jax.ShapeDtypeStruct(grid.shape, jnp.float32),
+            jax.ShapeDtypeStruct((3, groups, width), jnp.float32),
             jax.ShapeDtypeStruct((1, 128), jnp.float32),
         ],
-        in_specs=[vmem] * (1 + len(tables)),
+        in_specs=[vmem] * (4 + len(tables)),
         out_specs=[vmem] * 2,
         scratch_shapes=[
-            blocks, blocks, blocks, blocks,
-            pltpu.VMEM((16 * KX, 128), jnp.float32),
-            pltpu.VMEM((count, 1, 128), jnp.float32),
-            pltpu.VMEM((1, 128), jnp.float32),
-        ] + [pltpu.SemaphoreType.DMA((count,))] * 6,
+            held(block_x + 8, block_y + 8, KZ),
+            held(block_x + 8, block_y + 8, KZ),
+            *weight_scratch(groups, width),
+            *weight_scratch(groups, width),
+            traffic, traffic, traffic, traffic,
+            held(16 * KX, 128),
+            held(count, 1, 128),
+            held(1, 128),
+            held(slabs, depth, 8, KZ), held(5, block_y, KZ), held(5, 8, KZ),
+            held(slabs, depth, 8, KZ), held(5, block_y, KZ), held(5, 8, KZ),
+            dma((slabs, count)), dma((slabs, count)),
+            dma((slabs, count)), dma((slabs, count)),
+            dma((count,)), dma((count,)),
+            dma((slabs,)), dma((slabs,)), dma((slabs,)), dma((slabs,)),
+            dma((4,)), dma((4,)),
+        ],
         compiler_params=pltpu.CompilerParams(
             collective_id=1, has_side_effects=True, vmem_limit_bytes=60 * 1024 * 1024
         ),
-        name="slab",
-    )(grid, *tables)
-    return (potential, energy[0, 0])
-
-
-def slab_fits(grp, pen, block_x, block_y):
+        name="whole",
+    )(offsets, zcell, fracs, live_q, *tables)
+    return (forces, energy[0, 0])
+
+
+def slab_fits(grp, pen, slabs, block_x, block_y, per_row):
     fan = 128 // block_y
     return (
-        grp * pen * 8 == KZ and KX == KY and KY == KZ and pen % fan == 0
-        and block_x % (2 * fan) == 0 and KZ == 256
+        grp * pen * 8 == KZ and KX == KY and KY == KZ and KZ == 256 and pen % fan == 0
+        and block_x == 16 * slabs and 16 % (2 * fan) == 0 and per_row * 8 == block_y
     )
 
 
@@ -700,6 +883,10 @@
     offsets = cell_offsets.reshape(2, groups, width)
     zcell = cell_z.reshape(groups, width)
     fracs = frac.reshape(3, groups, width)
+    grp, pen = lax.axis_size("grp"), lax.axis_size("pen")
+    if slab_fits(grp, pen, 4, block_x, block_y, per_row):
+        forces, total = whole_program(offsets, zcell, fracs, live_q, slots, grp, pen, 4)
+        return (forces.reshape(3, groups * width), total / ATOMS)
     vmem = pl.BlockSpec(memory_space=pltpu.VMEM)
     params = pltpu.CompilerParams(vmem_limit_bytes=60 * 1024 * 1024)
     padded = pl.pallas_call(
@@ -715,11 +902,7 @@
     merged = padded[: block_x + 5, :block_y].at[:, :5].add(rim_y)
     rim_x = shifted(merged[block_x : block_x + 5], "grp", 1)
     grid = merged[:block_x] + jnp.pad(rim_x, ((0, block_x - 5), (0, 0), (0, 0)))
-    grp, pen = lax.axis_size("grp"), lax.axis_size("pen")
-    if slab_fits(grp, pen, block_x, block_y):
-        potential, total = slab_potential(grid, grp, pen)
-    else:
-        potential, total = spectrum_of(grid, block_x, block_y)
+    potential, total = spectrum_of(grid, block_x, block_y)
     upper = shifted(potential[:5], "grp", -1)
     ext_x = jnp.concatenate([potential[:, :5], upper[:, :5]], axis=0)
     beside = shifted(ext_x, "pen", -1)

time: 213 us -> 157 us (0.74)
  the two profiles are of different devices: /device:TPU:1 before, /device:TPU:17 now
where the time goes in v3:
time: 157 us; the launch traced here: 156 us
  Pallas kernels  147 us (94%)
  local copies, waits for them, and re-layouts  7.21 us (5%)
  between operations  1.88 us (1%)
    pallas_call x1, Pallas kernels, whole_program(): pl.pallas_call(functools.partial(whole_kernel, grp, pen, slots), out_shap...  147 us
    unnamed x15, local copies, waits for them, and re-layouts  6.12 us

profile of v3, /device:TPU:17, one launch (start us, length us, event | category | flops | bytes accessed | tf_op | source)
XLA Modules:
  0.0 156.4 jit_solution(13166316732399477757)
XLA Ops:
  0.6 0.0 copy-start.4
  0.6 0.1 lt.23
  0.7 0.6 copy-done.4
  1.3 0.1 lt.25
  1.4 0.1 copy.17
  1.5 0.0 copy-start.2
  1.5 0.1 copy.18
  1.6 0.8 copy-done.2
  2.4 0.0 copy-start.3
  2.4 0.7 reshape.29.cell_ref
  3.1 0.2 copy-done.3
  3.4 0.0 copy-start.1
  3.4 0.0 copy-start
  3.4 0.7 compare_select_fusion.q_ref
  4.1 0.2 copy-done.1
  4.3 0.7 copy.25
  5.0 0.0 copy-done
  5.0 0.8 copy.24
  5.8 146.6 %whole.1 = (f32[3,128,256]{2,1,0:T(8,128)}, f32[1,128]{1,0:T(1,128)}) custom-call(s32[2,128,256]{2,1,0:T(8,128)} %bitcast.14, s32[128,256]{1,0:T(8,128)} %reshape.29.cell_ref, f32[3,128,256]{2,1,0:T(8,128)} %bitcast.13, f32[128,256]{1,0:T(8,128)} %compare_select_fusion.q_ref, bf16[256,256]{1,0:T(8,128)(2,1)} %constant.26.clone.cas_hi, ...), custom_call_target="tpu_custom_call" | custom-call | tf_op jit(solution)/shard_map/whole/pallas_call | solution.py:832
  152.5 0.0 copy-start.5
  152.5 0.7 copy-done.5
  153.2 2.1 %copy.21 = f32[1,3,128,256]{3,1,2,0:T(4,128)} copy(f32[1,3,128,256]{3,2,1,0:T(8,128)} %bitcast.18) | data formatting | bytes 786432
  (3 shorter events, 0.1 us)
Async XLA Ops:
  0.6 0.7 copy-start.4
  1.5 0.9 copy-start.2
  2.4 0.9 copy-start.3
  3.4 0.9 copy-start.1
  3.4 1.6 %copy-start = (f32[3,32768]{1,0:T(4,128)S(1)}, f32[3,32768]{1,0:T(4,128)}, u32[]{:S(2)}) copy-start(f32[3,32768]{1,0:T(4,128)} %param.17) | copy-start | bytes 1179652
  152.5 0.7 copy-start.5

commit v4 on v3

--- a/solution.py
+++ b/solution.py
@@ -130,6 +130,16 @@
     return one(left[0], right[0]) + one(left[0], right[1]) + one(left[1], right[0])
 
 
+def stacked_dot(left, right, left_dim, right_dim):
+    dims = (((left_dim,), (right_dim,)), ((), ()))
+    one = functools.partial(
+        lax.dot_general, dimension_numbers=dims, preferred_element_type=jnp.float32
+    )
+    rows = left[0].shape[0]
+    both = one(jnp.concatenate(left, axis=0), right[0])
+    return both[:rows] + both[rows:] + one(left[0], right[1])
+
+
 def spread_row(a, per_row, cell_ref, q_ref, x_ref, y_ref, z_ref, grid_ref):
     groups, width = cell_ref.shape
     outs = []
@@ -140,7 +150,7 @@
         weights = z_weights(z_masks(base), z_window(base, values))
         along_y = rows_of_y(y_ref, group, groups, width) * q_ref[pl.ds(group, 1), :]
         pair = [x_ref[k, pl.ds(group, 1), :] * along_y for k in range(7)]
-        outs.append(dot3(split(jnp.concatenate(pair, axis=0)), weights, 1, 1))
+        outs.append(stacked_dot(split(jnp.concatenate(pair, axis=0)), weights, 1, 1))
     for k in range(7):
         for t in range(per_row + 1):
             value = 0.0
@@ -180,8 +190,9 @@
         grade_y = rows_of_y(slope[1], group, groups, width)
         minus_q = -q_ref[row, :]
         pieces = (along_x * weight_y, along_y * grade_y, along_z * weight_y)
-        for d, piece in enumerate(pieces):
-            out_ref[d, row, :] = minus_q * jnp.sum(piece, axis=0, keepdims=True)
+        sums = [jnp.sum(piece, axis=0, keepdims=True) for piece in pieces]
+        lanes = pl.ds(pl.multiple_of(group * width, width), width)
+        out_ref[:, lanes] = minus_q * jnp.concatenate(sums, axis=0)
 
 
 def weight_scratch(groups, width):
@@ -489,7 +500,7 @@
 
 
 def whole_kernel(
-    grp, pen, slots, off_ref, cell_ref, frac_ref, q_ref, cas_hi, cas_lo, into_hi, into_lo,
+    grp, pen, slots, sizes, off_ref, cell_ref, frac_ref, q_ref, cas_hi, cas_lo, into_hi, into_lo,
     back_hi, back_lo, factor_row, factor_col, square_row, square_col, out_ref, energy_ref,
     pad, ext, plain_x, plain_y, plain_z, slope_x, slope_y, slope_z,
     send, recv, send_back, recv_back, work, sums, part,
@@ -498,16 +509,14 @@
     side_send, side_recv, halo_send, halo_recv, edge_send, edge_recv,
 ):
     count = grp * pen
-    slabs, blocks = send.shape[0], send.shape[2]
+    slabs = len(sizes)
+    starts = [sum(sizes[:s]) for s in range(slabs)]
     groups = cell_ref.shape[0]
     block_x, block_y = KX // grp, KY // pen
     tile_rows = block_x // 2
     per_row = groups // tile_rows
     fan = 128 // block_y
-    depth = block_x // slabs
-    step = depth // 2
     half = pen // fan
-    lines = 8 * blocks
     at_grp, at_pen = lax.axis_index("grp"), lax.axis_index("pen")
     me = at_grp * pen + at_pen
     plain = (plain_x, plain_y, plain_z)
@@ -545,31 +554,31 @@
 
         lax.fori_loop(1, count, one, 0)
 
-    def out_copy(s):
+    def slab_copy(s, source, target, sems):
+        part_of = pl.ds(starts[s], sizes[s])
+
         def make(d):
             peer, where = peer_of(d)
-            sems = (out_send.at[s, d], out_recv.at[s, d])
-            return remote(send.at[s, peer], recv.at[s, me], sems, where)
+            pair = (sems[0].at[s, d], sems[1].at[s, d])
+            return remote(source.at[peer, part_of], target.at[me, part_of], pair, where)
 
         return make
 
+    def out_copy(s):
+        return slab_copy(s, send, recv, (out_send, out_recv))
+
     def back_copy(s):
-        def make(d):
-            peer, where = peer_of(d)
-            sems = (back_send.at[s, d], back_recv.at[s, d])
-            return remote(send_back.at[s, peer], recv_back.at[s, me], sems, where)
-
-        return make
+        return slab_copy(s, send_back, recv_back, (back_send, back_recv))
 
     def sum_copy(d):
         return remote(part, sums.at[me], (sum_send.at[d], sum_recv.at[d]), peer_of(d)[1])
 
     def slab_rows(s):
-        return pl.ds(s * depth, depth)
+        return pl.ds(starts[s] * fan, sizes[s] * fan)
 
     def side_rim(s):
         source = pad.at[slab_rows(s), pl.ds(block_y, 8), :]
-        return remote(source, rim_side.at[s], (side_send.at[s], side_recv.at[s]), device(0, 1))
+        return remote(source, rim_side.at[slab_rows(s)], (side_send.at[s], side_recv.at[s]), device(0, 1))
 
     def edge_rims():
         source = pad.at[pl.ds(block_x, 5)]
@@ -586,7 +595,7 @@
 
     def side_halo(s):
         source = ext.at[slab_rows(s), pl.ds(0, 8), :]
-        return remote(source, halo_side.at[s], (halo_send.at[s], halo_recv.at[s]), device(0, -1))
+        return remote(source, halo_side.at[slab_rows(s)], (halo_send.at[s], halo_recv.at[s]), device(0, -1))
 
     def edge_halos():
         source = ext.at[pl.ds(0, 5)]
@@ -612,48 +621,57 @@
     lax.fori_loop(1, count, greet, 0)
     pad[...] = jnp.zeros_like(pad)
 
-    def prepare(outer, carry):
-        store_weights(outer, slots, off_ref, frac_ref, *plain, 0)
-        return carry
-
-    lax.fori_loop(0, groups // 8, prepare, 0)
     pl.semaphore_wait(barrier, count - 1)
 
     def ship(s):
         side_rim(s).wait_recv()
-        pad[slab_rows(s), pl.ds(0, 8), :] += rim_side[s]
+        pad[slab_rows(s), pl.ds(0, 8), :] += rim_side[slab_rows(s)]
 
     def transform_out(s):
         def along_z(i, carry):
-            rows = pad[pl.ds(s * depth + 2 * fan * i, 2 * fan), pl.ds(0, block_y), :]
+            tile = starts[s] + 2 * i
+            rows = pad[pl.ds(tile * fan, 2 * fan), pl.ds(0, block_y), :]
             out = dot3(cas, split(rows.reshape(256, KZ)), 1, 1)
             for t in range(2):
                 block = out[:, 128 * t : 128 * t + 128].reshape(count, 8, 128)
-                send[s, :, 2 * i + t] = block
+                send[:, tile + t] = block
             return carry
 
-        lax.fori_loop(0, blocks // 2, along_z, 0)
+        lax.fori_loop(0, sizes[s] // 2, along_z, 0)
         fan_out(out_copy(s))
-        recv[s, me] = send[s, me]
+        own = pl.ds(starts[s], sizes[s])
+        recv[me, own] = send[me, own]
+
+    ready = [max((start * fan - 5) // 2, 0) for start in starts]
+    rows_per_outer = 8 // per_row
 
     def spread_step(i, carry):
         a = tile_rows - 1 - i
+
+        @pl.when(lax.rem(i, rows_per_outer) == 0)
+        def _():
+            outer = lax.div(a, rows_per_outer)
+            store_weights(outer, slots, off_ref, frac_ref, *plain, 0)
+
         spread_row(a, per_row, cell_ref, q_ref, *plain, pad)
 
-        @pl.when(((lax.rem(a + 3, step) == 0) & (a + 3 < tile_rows)) | (a == 0))
-        def _():
-            side_rim(lax.div(a + 3, step)).start()
-
-        @pl.when(a == tile_rows - step - 3)
+        @pl.when(a == tile_rows - 3)
         def _():
             for copy in edge_rims():
                 copy.start()
 
-        @pl.when((lax.rem(a + 7, step) == 0) & (a + 7 < tile_rows))
-        def _():
-            s = lax.div(a + 7, step)
-            ship(s)
-            transform_out(s)
+        for s in range(slabs):
+
+            @pl.when(a == ready[s])
+            def _(s=s):
+                side_rim(s).start()
+
+            if s:
+
+                @pl.when(a == max(ready[s] - 5, 0))
+                def _(s=s):
+                    ship(s)
+                    transform_out(s)
 
         return carry
 
@@ -671,27 +689,27 @@
 
     lax.fori_loop(0, groups // 8, prepare_slopes, 0)
 
-    def along_y(i, carry):
-        s = slabs - 1 - i
+    def slab_lines(s, h):
+        span = sizes[s] * 8 * KX // (block_x // fan)
+        return pl.ds(starts[s] * 8 * KX // (block_x // fan) + h * 8 * KX, span)
+
+    for s in reversed(range(slabs)):
         fan_wait(out_copy(s), True)
         rows = []
+        own = pl.ds(starts[s], sizes[s])
         for g in range(grp):
             parts = [[] for _ in range(fan)]
             for h in range(half):
                 loaded = [
-                    recv[s, g * pen + h * fan + k].reshape(lines, 128) for k in range(fan)
+                    recv[g * pen + h * fan + k, own].reshape(8 * sizes[s], 128)
+                    for k in range(fan)
                 ]
                 for k, tile in enumerate(regroup(loaded, block_y)):
                     parts[k].append(tile)
-            rows += [jnp.concatenate(part, axis=1) for part in parts]
+            rows += [jnp.concatenate(pieces, axis=1) for pieces in parts]
         out = dot3(split(jnp.concatenate(rows, axis=0)), cas, 1, 0)
-        span = grp * fan * lines
         for h in range(2):
-            start = pl.multiple_of(s * span + h * 8 * KX, 128)
-            work[pl.ds(start, span), :] = out[:, 128 * h : 128 * h + 128]
-        return carry
-
-    lax.fori_loop(0, slabs, along_y, 0)
+            work[slab_lines(s, h), :] = out[:, 128 * h : 128 * h + 128]
 
     scale = 1.0 / (math.pi * KX * KY * KZ)
     first = pl.multiple_of(8 * me, 8)
@@ -699,38 +717,36 @@
     square_z = square_col[pl.ds(first, 8), :]
     pick = lax.broadcasted_iota(jnp.int32, (8, 1), 0)
 
-    def along_x(f, total):
-        fz = jnp.sum(jnp.where(pick == f, factor_z, 0.0), axis=0, keepdims=True) * scale
-        sz = jnp.sum(jnp.where(pick == f, square_z, 0.0), axis=0, keepdims=True)
-        rows = jnp.concatenate(
-            [work[pl.ds(f + h * 8 * KX, KX, stride=8), :] for h in range(2)], axis=1
-        )
-        spectrum = dot3((into_hi[...], into_lo[...]), split(rows), 1, 0)
-        square = square_col[...] + (square_row[...] + sz)
-        safe = jnp.where(square > 0, square, 1.0)
-        kernel = factor_col[...] * (factor_row[...] * fz) / safe
-        kernel = jnp.where(square > 0, kernel, 0.0)
-        scaled = kernel * spectrum
-        total = total + jnp.sum(scaled * spectrum, axis=0, keepdims=True)
-        out = dot3((back_hi[...], back_lo[...]), split(scaled), 1, 0)
-        for h in range(2):
-            work[pl.ds(f + h * 8 * KX, KX, stride=8), :] = out[:, 128 * h : 128 * h + 128]
+    def along_x(i, total):
+        for f in (2 * i, 2 * i + 1):
+            chosen = pick == f
+            fz = jnp.sum(jnp.where(chosen, factor_z, 0.0), axis=0, keepdims=True) * scale
+            sz = jnp.sum(jnp.where(chosen, square_z, 0.0), axis=0, keepdims=True)
+            rows = jnp.concatenate(
+                [work[pl.ds(f + h * 8 * KX, KX, stride=8), :] for h in range(2)], axis=1
+            )
+            spectrum = dot3((into_hi[...], into_lo[...]), split(rows), 1, 0)
+            square = square_col[...] + (square_row[...] + sz)
+            safe = jnp.where(square > 0, square, 1.0)
+            kernel = factor_col[...] * (factor_row[...] * fz) / safe
+            kernel = jnp.where(square > 0, kernel, 0.0)
+            scaled = kernel * spectrum
+            total = total + jnp.sum(scaled * spectrum, axis=0, keepdims=True)
+            out = dot3((back_hi[...], back_lo[...]), split(scaled), 1, 0)
+            for h in range(2):
+                rows = pl.ds(f + h * 8 * KX, KX, stride=8)
+                work[rows, :] = out[:, 128 * h : 128 * h + 128]
         return total
 
-    total = lax.fori_loop(0, 8, along_x, jnp.zeros((1, KY), jnp.float32))
+    total = lax.fori_loop(0, 4, along_x, jnp.zeros((1, KY), jnp.float32))
     part[...] = jnp.broadcast_to(0.5 * jnp.sum(total, axis=1, keepdims=True), (1, 128))
     sums[me] = part[...]
 
-    def back_y(s, carry):
-        span = grp * fan * lines
-        rows = jnp.concatenate(
-            [
-                work[pl.ds(pl.multiple_of(s * span + h * 8 * KX, 128), span), :]
-                for h in range(2)
-            ],
-            axis=1,
-        )
+    for s in range(slabs):
+        rows = jnp.concatenate([work[slab_lines(s, h), :] for h in range(2)], axis=1)
         out = dot3(split(rows), cas, 1, 0)
+        lines = 8 * sizes[s]
+        own = pl.ds(starts[s], sizes[s])
         for g in range(grp):
             for h in range(half):
                 parts = []
@@ -738,49 +754,49 @@
                     start = (g * fan + k) * lines
                     parts.append(out[start : start + lines, 128 * h : 128 * h + 128])
                 for k, tile in enumerate(regroup(parts, block_y)):
-                    send_back[s, g * pen + h * fan + k] = tile.reshape(blocks, 8, 128)
+                    send_back[g * pen + h * fan + k, own] = tile.reshape(sizes[s], 8, 128)
         fan_out(back_copy(s))
-        recv_back[s, me] = send_back[s, me]
-        return carry
-
-    lax.fori_loop(0, slabs, back_y, 0)
+        recv_back[me, own] = send_back[me, own]
     fan_out(sum_copy)
 
-    def home(s, carry):
+    def home(s):
         fan_wait(back_copy(s), True)
 
         def home_z(i, inner):
+            tile = starts[s] + 2 * i
             rows = jnp.concatenate(
-                [recv_back[s, :, 2 * i + t].reshape(KZ, 128) for t in range(2)], axis=1
+                [recv_back[:, tile + t].reshape(KZ, 128) for t in range(2)], axis=1
             )
             out = dot3(split(jnp.transpose(rows)), cas, 1, 0)
-            where = pl.ds(s * depth + 2 * fan * i, 2 * fan)
+            where = pl.ds(tile * fan, 2 * fan)
             ext[where, pl.ds(0, block_y), :] = out.reshape(2 * fan, block_y, KZ)
             return inner
 
-        lax.fori_loop(0, blocks // 2, home_z, 0)
+        lax.fori_loop(0, sizes[s] // 2, home_z, 0)
         side_halo(s).start()
-        return carry
-
-    home(0, 0)
+
+    def join_halo(s):
+        side_halo(s).wait_recv()
+        ext[slab_rows(s), pl.ds(block_y, 8), :] = halo_side[slab_rows(s)]
+
+    home(0)
     for copy in edge_halos():
         copy.start()
-    home(1, 0)
-
-    def join_halo(s):
-        side_halo(s).wait_recv()
-        ext[slab_rows(s), pl.ds(block_y, 8), :] = halo_side[s]
-
     join_halo(0)
+    needed = [max((start * fan - 5) // 2, 0) for start in starts]
+    early = [0] + [min(needed[s], 3) for s in range(1, slabs)]
+    early[-1] = min(needed[-1], 5)
 
     def interp_step(a, carry):
-        @pl.when((lax.rem(a, step) == 0) & (a >= step) & (a < tile_rows - step))
-        def _():
-            home(lax.div(a, step) + 1, 0)
-
-        @pl.when((lax.rem(a + 3, step) == 0) & (a + 3 < tile_rows))
-        def _():
-            join_halo(lax.div(a + 3, step))
+        for s in range(1, slabs):
+
+            @pl.when(a == needed[s] - early[s])
+            def _(s=s):
+                home(s)
+
+            @pl.when(a == needed[s])
+            def _(s=s):
+                join_halo(s)
 
         @pl.when(a == tile_rows - 3)
         def _():
@@ -797,27 +813,29 @@
     energy_ref[...] = jnp.sum(sums[...], axis=0)
     fan_wait(sum_copy, False)
 
-    def drain(s, carry):
+    for s in range(slabs):
         fan_wait(out_copy(s), False)
         fan_wait(back_copy(s), False)
         side_rim(s).wait_send()
         side_halo(s).wait_send()
-        return carry
-
-    lax.fori_loop(0, slabs, drain, 0)
     for copy in edge_rims() + edge_halos():
         copy.wait_send()
 
 
-def whole_program(offsets, zcell, fracs, live_q, slots, grp, pen, slabs):
+def whole_program(offsets, zcell, fracs, live_q, slots, grp, pen, sizes):
     count = grp * pen
     groups, width = zcell.shape
     block_x, block_y = KX // grp, KY // pen
     fan = 128 // block_y
-    blocks = block_x // fan // slabs
-    depth = block_x // slabs
+    slabs = len(sizes)
     cas = cas_table(KZ)
-    order = np.arange(KX).reshape(grp, slabs, blocks, fan).transpose(1, 0, 3, 2).reshape(KX)
+    cells = np.arange(KX).reshape(grp, block_x // fan, fan)
+    order = np.concatenate(
+        [
+            cells[:, sum(sizes[:s]) : sum(sizes[: s + 1])].transpose(0, 2, 1).reshape(-1)
+            for s in range(slabs)
+        ]
+    )
     factor, square = spline_factor(KX)
     tables = [*halves(cas), *halves(cas[:, order]), *halves(cas[order, :])]
     tables += [factor[None, :], factor[:, None], square[None, :], square[:, None]]
@@ -827,12 +845,12 @@
     def held(*shape):
         return pltpu.VMEM(shape, jnp.float32)
 
-    traffic = held(slabs, count, blocks, 8, 128)
+    traffic = held(count, block_x // fan, 8, 128)
     dma = pltpu.SemaphoreType.DMA
     forces, energy = pl.pallas_call(
-        functools.partial(whole_kernel, grp, pen, slots),
+        functools.partial(whole_kernel, grp, pen, slots, sizes),
         out_shape=[
-            jax.ShapeDtypeStruct((3, groups, width), jnp.float32),
+            jax.ShapeDtypeStruct((3, groups * width), jnp.float32),
             jax.ShapeDtypeStruct((1, 128), jnp.float32),
         ],
         in_specs=[vmem] * (4 + len(tables)),
@@ -846,8 +864,8 @@
             held(16 * KX, 128),
             held(count, 1, 128),
             held(1, 128),
-            held(slabs, depth, 8, KZ), held(5, block_y, KZ), held(5, 8, KZ),
-            held(slabs, depth, 8, KZ), held(5, block_y, KZ), held(5, 8, KZ),
+            held(block_x, 8, KZ), held(5, block_y, KZ), held(5, 8, KZ),
+            held(block_x, 8, KZ), held(5, block_y, KZ), held(5, 8, KZ),
             dma((slabs, count)), dma((slabs, count)),
             dma((slabs, count)), dma((slabs, count)),
             dma((count,)), dma((count,)),
@@ -862,11 +880,11 @@
     return (forces, energy[0, 0])
 
 
-def slab_fits(grp, pen, slabs, block_x, block_y, per_row):
+def slab_fits(grp, pen, sizes, block_x, block_y, per_row):
     fan = 128 // block_y
     return (
         grp * pen * 8 == KZ and KX == KY and KY == KZ and KZ == 256 and pen % fan == 0
-        and block_x == 16 * slabs and 16 % (2 * fan) == 0 and per_row * 8 == block_y
+        and block_x == fan * sum(sizes) and per_row * 8 == block_y and 8 % per_row == 0
     )
 
 
@@ -884,9 +902,10 @@
     zcell = cell_z.reshape(groups, width)
     fracs = frac.reshape(3, groups, width)
     grp, pen = lax.axis_size("grp"), lax.axis_size("pen")
-    if slab_fits(grp, pen, 4, block_x, block_y, per_row):
-        forces, total = whole_program(offsets, zcell, fracs, live_q, slots, grp, pen, 4)
-        return (forces.reshape(3, groups * width), total / ATOMS)
+    sizes = (4, 6, 4, 2)
+    if slab_fits(grp, pen, sizes, block_x, block_y, per_row):
+        forces, total = whole_program(offsets, zcell, fracs, live_q, slots, grp, pen, sizes)
+        return (forces, total / ATOMS)
     vmem = pl.BlockSpec(memory_space=pltpu.VMEM)
     params = pltpu.CompilerParams(vmem_limit_bytes=60 * 1024 * 1024)
     padded = pl.pallas_call(
@@ -909,7 +928,7 @@
     beside = jnp.pad(beside, ((0, 0), (0, 3), (0, 0)))
     forces = pl.pallas_call(
         functools.partial(interp_kernel, per_row, slots),
-        out_shape=jax.ShapeDtypeStruct((3, groups, width), jnp.float32),
+        out_shape=jax.ShapeDtypeStruct((3, groups * width), jnp.float32),
         in_specs=[vmem] * 7,
         out_specs=vmem,
         scratch_shapes=[pltpu.VMEM((block_x + 8, block_y + 8, KZ), jnp.float32)]
@@ -917,7 +936,7 @@
         compiler_params=params,
         name="interp",
     )(offsets, zcell, fracs, live_q, potential, upper, beside)
-    return (forces.reshape(3, groups * width), total / ATOMS)
+    return (forces, total / ATOMS)
 
 
 def solution(mesh):

time: 157 us -> 155 us (0.987)
  the two profiles are of different devices: /device:TPU:17 before, /device:TPU:19 now
where the time goes in v4:
time: 155 us
  Pallas kernels  145 us (94%)
  local copies, waits for them, and re-layouts  7.02 us (5%)
  between operations  1.88 us (1%)
    pallas_call x1, Pallas kernels, whole_program(): pl.pallas_call(functools.partial(whole_kernel, grp, pen, slots, sizes), o...  145 us
    unnamed x15, local copies, waits for them, and re-layouts  5.93 us

profile of v4, /device:TPU:19, one launch (start us, length us, event | category | flops | bytes accessed | tf_op | source)
XLA Modules:
  0.0 154.7 jit_solution(16624735390259715272)
XLA Ops:
  0.6 0.0 copy-start.4
  0.6 0.1 lt.23
  0.7 0.6 copy-done.4
  1.3 0.1 lt.25
  1.4 0.1 copy.17
  1.5 0.0 copy-start.2
  1.5 0.1 copy.18
  1.6 0.8 copy-done.2
  2.4 0.0 copy-start.3
  2.4 0.7 reshape.26.cell_ref
  3.1 0.2 copy-done.3
  3.4 0.0 copy-start.1
  3.4 0.0 copy-start
  3.4 0.7 compare_select_fusion.q_ref
  4.1 0.2 copy-done.1
  4.3 0.7 copy.24
  5.0 0.0 copy-done
  5.0 0.8 copy.23
  5.8 145.2 %whole.1 = (f32[3,32768]{1,0:T(4,128)}, f32[1,128]{1,0:T(1,128)}) custom-call(s32[2,128,256]{2,1,0:T(8,128)} %bitcast.12, s32[128,256]{1,0:T(8,128)} %reshape.26.cell_ref, f32[3,128,256]{2,1,0:T(8,128)} %bitcast.11, f32[128,256]{1,0:T(8,128)} %compare_select_fusion.q_ref, bf16[256,256]{1,0:T(8,128)(2,1)} %constant.26.clone.cas_hi, ...), custom_call_target="tpu_custom_call" | custom-call | tf_op jit(solution)/shard_map/whole/pallas_call | solution.py:850
  151.0 0.0 copy-start.5
  151.0 0.6 copy-done.5
  151.7 1.9 %copy.26 = f32[3,32768]{1,0:T(4,128)} copy(f32[3,32768]{1,0:T(4,128)} %get-tuple-element.8) | data formatting | bytes 786432
  (3 shorter events, 0.1 us)
Async XLA Ops:
  0.6 0.7 copy-start.4
  1.5 0.9 copy-start.2
  2.4 0.9 copy-start.3
  3.4 0.9 copy-start.1
  3.4 1.6 %copy-start = (f32[3,32768]{1,0:T(4,128)S(1)}, f32[3,32768]{1,0:T(4,128)}, u32[]{:S(2)}) copy-start(f32[3,32768]{1,0:T(4,128)} %param.17) | copy-start | bytes 1179652
  151.0 0.6 copy-start.5

commit v5 on v4

--- a/solution.py
+++ b/solution.py
@@ -539,30 +539,29 @@
         peer = lax.rem(me + d, count)
         return (peer, {"grp": lax.div(peer, pen), "pen": lax.rem(peer, pen)})
 
+    first_hop = pen * (grp // 2 - lax.rem(at_grp, grp // 2))
+
     def fan_out(make):
         def one(e, carry):
-            make(1 + lax.rem(e + pen - 1, count - 1)).start()
+            make(1 + lax.rem(e + first_hop - 1, count - 1)).start()
             return carry
 
         lax.fori_loop(0, count - 1, one, 0)
 
-    def fan_wait(make, receiving):
-        def one(d, carry):
-            copy = make(d)
-            copy.wait_recv() if receiving else copy.wait_send()
-            return carry
-
-        lax.fori_loop(1, count, one, 0)
+    others = pl.ds(0, count - 1)
 
     def slab_copy(s, source, target, sems):
         part_of = pl.ds(starts[s], sizes[s])
+        pair = (sems[0].at[s], sems[1].at[s])
 
         def make(d):
             peer, where = peer_of(d)
-            pair = (sems[0].at[s, d], sems[1].at[s, d])
             return remote(source.at[peer, part_of], target.at[me, part_of], pair, where)
 
-        return make
+        total = remote(
+            source.at[others, part_of], target.at[others, part_of], pair, peer_of(1)[1]
+        )
+        return (make, total)
 
     def out_copy(s):
         return slab_copy(s, send, recv, (out_send, out_recv))
@@ -570,8 +569,10 @@
     def back_copy(s):
         return slab_copy(s, send_back, recv_back, (back_send, back_recv))
 
-    def sum_copy(d):
-        return remote(part, sums.at[me], (sum_send.at[d], sum_recv.at[d]), peer_of(d)[1])
+    def sum_copy():
+        pair = (sum_send.at[0], sum_recv.at[0])
+        total = remote(sums.at[others], sums.at[others], pair, peer_of(1)[1])
+        return (lambda d: remote(part, sums.at[me], pair, peer_of(d)[1]), total)
 
     def slab_rows(s):
         return pl.ds(starts[s] * fan, sizes[s] * fan)
@@ -621,8 +622,6 @@
     lax.fori_loop(1, count, greet, 0)
     pad[...] = jnp.zeros_like(pad)
 
-    pl.semaphore_wait(barrier, count - 1)
-
     def ship(s):
         side_rim(s).wait_recv()
         pad[slab_rows(s), pl.ds(0, 8), :] += rim_side[slab_rows(s)]
@@ -638,14 +637,14 @@
             return carry
 
         lax.fori_loop(0, sizes[s] // 2, along_z, 0)
-        fan_out(out_copy(s))
+        fan_out(out_copy(s)[0])
         own = pl.ds(starts[s], sizes[s])
         recv[me, own] = send[me, own]
 
     ready = [max((start * fan - 5) // 2, 0) for start in starts]
     rows_per_outer = 8 // per_row
 
-    def spread_step(i, carry):
+    def spread_plain(i, carry):
         a = tile_rows - 1 - i
 
         @pl.when(lax.rem(i, rows_per_outer) == 0)
@@ -654,8 +653,13 @@
             store_weights(outer, slots, off_ref, frac_ref, *plain, 0)
 
         spread_row(a, per_row, cell_ref, q_ref, *plain, pad)
-
-        @pl.when(a == tile_rows - 3)
+        return carry
+
+    def spread_step(i, carry):
+        a = tile_rows - 1 - i
+        spread_plain(i, carry)
+
+        @pl.when(a == ready[-1])
         def _():
             for copy in edge_rims():
                 copy.start()
@@ -675,7 +679,10 @@
 
         return carry
 
-    lax.fori_loop(0, tile_rows, spread_step, 0)
+    alone = tile_rows - 1 - ready[-1]
+    lax.fori_loop(0, alone, spread_plain, 0)
+    pl.semaphore_wait(barrier, count - 1)
+    lax.fori_loop(alone, tile_rows, spread_step, 0)
     for copy in edge_rims():
         copy.wait_recv()
     ship(0)
@@ -694,7 +701,7 @@
         return pl.ds(starts[s] * 8 * KX // (block_x // fan) + h * 8 * KX, span)
 
     for s in reversed(range(slabs)):
-        fan_wait(out_copy(s), True)
+        out_copy(s)[1].wait_recv()
         rows = []
         own = pl.ds(starts[s], sizes[s])
         for g in range(grp):
@@ -755,12 +762,15 @@
                     parts.append(out[start : start + lines, 128 * h : 128 * h + 128])
                 for k, tile in enumerate(regroup(parts, block_y)):
                     send_back[g * pen + h * fan + k, own] = tile.reshape(sizes[s], 8, 128)
-        fan_out(back_copy(s))
         recv_back[me, own] = send_back[me, own]
-    fan_out(sum_copy)
+        if s == 0:
+            fan_out(back_copy(s)[0])
+    fan_out(sum_copy()[0])
 
     def home(s):
-        fan_wait(back_copy(s), True)
+        back_copy(s)[1].wait_recv()
+        if s + 1 < slabs:
+            fan_out(back_copy(s + 1)[0])
 
         def home_z(i, inner):
             tile = starts[s] + 2 * i
@@ -782,7 +792,6 @@
     home(0)
     for copy in edge_halos():
         copy.start()
-    join_halo(0)
     needed = [max((start * fan - 5) // 2, 0) for start in starts]
     early = [0] + [min(needed[s], 3) for s in range(1, slabs)]
     early[-1] = min(needed[-1], 5)
@@ -793,6 +802,8 @@
             @pl.when(a == needed[s] - early[s])
             def _(s=s):
                 home(s)
+
+        for s in range(slabs):
 
             @pl.when(a == needed[s])
             def _(s=s):
@@ -809,13 +820,13 @@
         return carry
 
     lax.fori_loop(0, tile_rows, interp_step, 0)
-    fan_wait(sum_copy, True)
+    sum_copy()[1].wait_recv()
     energy_ref[...] = jnp.sum(sums[...], axis=0)
-    fan_wait(sum_copy, False)
+    sum_copy()[1].wait_send()
 
     for s in range(slabs):
-        fan_wait(out_copy(s), False)
-        fan_wait(back_copy(s), False)
+        out_copy(s)[1].wait_send()
+        back_copy(s)[1].wait_send()
         side_rim(s).wait_send()
         side_halo(s).wait_send()
     for copy in edge_rims() + edge_halos():
@@ -866,9 +877,8 @@
             held(1, 128),
             held(block_x, 8, KZ), held(5, block_y, KZ), held(5, 8, KZ),
             held(block_x, 8, KZ), held(5, block_y, KZ), held(5, 8, KZ),
-            dma((slabs, count)), dma((slabs, count)),
-            dma((slabs, count)), dma((slabs, count)),
-            dma((count,)), dma((count,)),
+            dma((slabs,)), dma((slabs,)), dma((slabs,)), dma((slabs,)),
+            dma((1,)), dma((1,)),
             dma((slabs,)), dma((slabs,)), dma((slabs,)), dma((slabs,)),
             dma((4,)), dma((4,)),
         ],
@@ -902,7 +912,7 @@
     zcell = cell_z.reshape(groups, width)
     fracs = frac.reshape(3, groups, width)
     grp, pen = lax.axis_size("grp"), lax.axis_size("pen")
-    sizes = (4, 6, 4, 2)
+    sizes = (6, 4, 4, 2)
     if slab_fits(grp, pen, sizes, block_x, block_y, per_row):
         forces, total = whole_program(offsets, zcell, fracs, live_q, slots, grp, pen, sizes)
         return (forces, total / ATOMS)

time: 155 us -> 145 us (0.935)
  the two profiles are of different devices: /device:TPU:19 before, /device:TPU:1 now
where the time goes in v5:
time: 145 us
  Pallas kernels  135 us (93%)
  local copies, waits for them, and re-layouts  7.02 us (5%)
  between operations  1.88 us (1%)
    pallas_call x1, Pallas kernels, whole_program(): pl.pallas_call(functools.partial(whole_kernel, grp, pen, slots, sizes), o...  135 us
    unnamed x15, local copies, waits for them, and re-layouts  5.93 us

profile of v5, /device:TPU:1, one launch (start us, length us, event | category | flops | bytes accessed | tf_op | source)
XLA Modules:
  0.0 144.5 jit_solution(9807014454202544090)
XLA Ops:
  0.6 0.0 copy-start.4
  0.6 0.1 lt.23
  0.7 0.6 copy-done.4
  1.3 0.1 lt.25
  1.4 0.1 copy.17
  1.5 0.0 copy-start.2
  1.5 0.1 copy.18
  1.6 0.8 copy-done.2
  2.4 0.0 copy-start.3
  2.4 0.7 reshape.26.cell_ref
  3.1 0.2 copy-done.3
  3.4 0.0 copy-start.1
  3.4 0.0 copy-start
  3.4 0.7 compare_select_fusion.q_ref
  4.1 0.2 copy-done.1
  4.3 0.7 copy.24
  5.0 0.0 copy-done
  5.0 0.8 copy.23
  5.8 135.0 %whole.1 = (f32[3,32768]{1,0:T(4,128)}, f32[1,128]{1,0:T(1,128)}) custom-call(s32[2,128,256]{2,1,0:T(8,128)} %bitcast.12, s32[128,256]{1,0:T(8,128)} %reshape.26.cell_ref, f32[3,128,256]{2,1,0:T(8,128)} %bitcast.11, f32[128,256]{1,0:T(8,128)} %compare_select_fusion.q_ref, bf16[256,256]{1,0:T(8,128)(2,1)} %constant.26.clone.cas_hi, ...), custom_call_target="tpu_custom_call" | custom-call | tf_op jit(solution)/shard_map/whole/pallas_call | solution.py:861
  140.8 0.0 copy-start.5
  140.8 0.6 copy-done.5
  141.5 1.9 %copy.26 = f32[3,32768]{1,0:T(4,128)} copy(f32[3,32768]{1,0:T(4,128)} %get-tuple-element.8) | data formatting | bytes 786432
  (3 shorter events, 0.1 us)
Async XLA Ops:
  0.6 0.7 copy-start.4
  1.5 0.9 copy-start.2
  2.4 0.9 copy-start.3
  3.4 0.9 copy-start.1
  3.4 1.6 %copy-start = (f32[3,32768]{1,0:T(4,128)S(1)}, f32[3,32768]{1,0:T(4,128)}, u32[]{:S(2)}) copy-start(f32[3,32768]{1,0:T(4,128)} %param.17) | copy-start | bytes 1179652
  140.8 0.6 copy-start.5

commit v6 on v5

--- a/solution.py
+++ b/solution.py
@@ -541,9 +541,13 @@
 
     first_hop = pen * (grp // 2 - lax.rem(at_grp, grp // 2))
 
-    def fan_out(make):
+    def fan_out(make, before=None):
         def one(e, carry):
-            make(1 + lax.rem(e + first_hop - 1, count - 1)).start()
+            d = 1 + lax.rem(e + first_hop - 1, count - 1)
+            if before is not None:
+                before(d).wait_send()
+            if make is not None:
+                make(d).start()
             return carry
 
         lax.fori_loop(0, count - 1, one, 0)
@@ -567,7 +571,18 @@
         return slab_copy(s, send, recv, (out_send, out_recv))
 
     def back_copy(s):
-        return slab_copy(s, send_back, recv_back, (back_send, back_recv))
+        part_of = pl.ds(starts[s], sizes[s])
+
+        def make(d):
+            peer, where = peer_of(d)
+            pair = (back_send.at[d], back_recv.at[s])
+            return remote(send_back.at[peer, part_of], recv_back.at[me, part_of], pair, where)
+
+        pair = (back_send.at[0], back_recv.at[s])
+        total = remote(
+            send_back.at[others, part_of], recv_back.at[others, part_of], pair, peer_of(1)[1]
+        )
+        return (make, total)
 
     def sum_copy():
         pair = (sum_send.at[0], sum_recv.at[0])
@@ -768,9 +783,9 @@
     fan_out(sum_copy()[0])
 
     def home(s):
+        if s + 1 < slabs:
+            fan_out(back_copy(s + 1)[0], back_copy(s)[0])
         back_copy(s)[1].wait_recv()
-        if s + 1 < slabs:
-            fan_out(back_copy(s + 1)[0])
 
         def home_z(i, inner):
             tile = starts[s] + 2 * i
@@ -826,7 +841,8 @@
 
     for s in range(slabs):
         out_copy(s)[1].wait_send()
-        back_copy(s)[1].wait_send()
+        if s + 1 == slabs:
+            fan_out(None, back_copy(s)[0])
         side_rim(s).wait_send()
         side_halo(s).wait_send()
     for copy in edge_rims() + edge_halos():
@@ -877,7 +893,7 @@
             held(1, 128),
             held(block_x, 8, KZ), held(5, block_y, KZ), held(5, 8, KZ),
             held(block_x, 8, KZ), held(5, block_y, KZ), held(5, 8, KZ),
-            dma((slabs,)), dma((slabs,)), dma((slabs,)), dma((slabs,)),
+            dma((slabs,)), dma((slabs,)), dma((count,)), dma((slabs,)),
             dma((1,)), dma((1,)),
             dma((slabs,)), dma((slabs,)), dma((slabs,)), dma((slabs,)),
             dma((4,)), dma((4,)),

time: 145 us -> 143 us (0.986)
  Pallas kernels: 135 us -> 133 us
    pallas_call x1, Pallas kernels: 135 us -> 133 us  [whole_program(): pl.pallas_call(functools.partial(whole_kernel, grp, pen, slots, sizes), o...]
where the time goes in v6:
time: 143 us
  Pallas kernels  133 us (93%)
  local copies, waits for them, and re-layouts  7.02 us (5%)
  between operations  1.88 us (1%)
    pallas_call x1, Pallas kernels, whole_program(): pl.pallas_call(functools.partial(whole_kernel, grp, pen, slots, sizes), o...  133 us
    unnamed x15, local copies, waits for them, and re-layouts  5.93 us

profile of v6, /device:TPU:1, one launch (start us, length us, event | category | flops | bytes accessed | tf_op | source)
XLA Modules:
  0.0 142.7 jit_solution(9951472702181664559)
XLA Ops:
  0.6 0.0 copy-start.4
  0.6 0.1 lt.23
  0.7 0.6 copy-done.4
  1.3 0.1 lt.25
  1.4 0.1 copy.17
  1.5 0.0 copy-start.2
  1.5 0.1 copy.18
  1.6 0.8 copy-done.2
  2.4 0.0 copy-start.3
  2.4 0.7 reshape.26.cell_ref
  3.1 0.2 copy-done.3
  3.4 0.0 copy-start.1
  3.4 0.0 copy-start
  3.4 0.7 compare_select_fusion.q_ref
  4.1 0.2 copy-done.1
  4.3 0.7 copy.24
  5.0 0.0 copy-done
  5.0 0.8 copy.23
  5.8 133.1 %whole.1 = (f32[3,32768]{1,0:T(4,128)}, f32[1,128]{1,0:T(1,128)}) custom-call(s32[2,128,256]{2,1,0:T(8,128)} %bitcast.12, s32[128,256]{1,0:T(8,128)} %reshape.26.cell_ref, f32[3,128,256]{2,1,0:T(8,128)} %bitcast.11, f32[128,256]{1,0:T(8,128)} %compare_select_fusion.q_ref, bf16[256,256]{1,0:T(8,128)(2,1)} %constant.26.clone.cas_hi, ...), custom_call_target="tpu_custom_call" | custom-call | tf_op jit(solution)/shard_map/whole/pallas_call | solution.py:877
  139.0 0.0 copy-start.5
  139.0 0.6 copy-done.5
  139.6 1.9 %copy.26 = f32[3,32768]{1,0:T(4,128)} copy(f32[3,32768]{1,0:T(4,128)} %get-tuple-element.8) | data formatting | bytes 786432
  (3 shorter events, 0.1 us)
Async XLA Ops:
  0.6 0.7 copy-start.4
  1.5 0.9 copy-start.2
  2.4 0.9 copy-start.3
  3.4 0.9 copy-start.1
  3.4 1.6 %copy-start = (f32[3,32768]{1,0:T(4,128)S(1)}, f32[3,32768]{1,0:T(4,128)}, u32[]{:S(2)}) copy-start(f32[3,32768]{1,0:T(4,128)} %param.17) | copy-start | bytes 1179652
  139.0 0.6 copy-start.5

commit v7 on v6

--- a/solution.py
+++ b/solution.py
@@ -130,6 +130,12 @@
     return one(left[0], right[0]) + one(left[0], right[1]) + one(left[1], right[0])
 
 
+def wide_row(ref, group, width):
+    parts = width // ref.shape[1]
+    rows = [ref[pl.ds(group * parts + i, 1), :] for i in range(parts)]
+    return rows[0] if parts == 1 else jnp.concatenate(rows, axis=1)
+
+
 def stacked_dot(left, right, left_dim, right_dim):
     dims = (((left_dim,), (right_dim,)), ((), ()))
     one = functools.partial(
@@ -141,14 +147,15 @@
 
 
 def spread_row(a, per_row, cell_ref, q_ref, x_ref, y_ref, z_ref, grid_ref):
-    groups, width = cell_ref.shape
+    groups, width = x_ref.shape[1:]
     outs = []
     for b in range(per_row):
         group = a * per_row + b
-        base = cell_ref[pl.ds(group, 1), :]
+        base = wide_row(cell_ref, group, width)
         values = [z_ref[j, pl.ds(group, 1), :] for j in range(6)]
         weights = z_weights(z_masks(base), z_window(base, values))
-        along_y = rows_of_y(y_ref, group, groups, width) * q_ref[pl.ds(group, 1), :]
+        along_y = rows_of_y(y_ref, group, groups, width)
+        along_y = along_y * wide_row(q_ref, group, width)
         pair = [x_ref[k, pl.ds(group, 1), :] * along_y for k in range(7)]
         outs.append(stacked_dot(split(jnp.concatenate(pair, axis=0)), weights, 1, 1))
     for k in range(7):
@@ -162,11 +169,11 @@
 
 
 def interp_row(a, per_row, cell_ref, q_ref, plain, slope, ext_ref, out_ref):
-    groups, width = cell_ref.shape
+    groups, width = plain[0].shape[1:]
     for b in range(per_row):
         group = a * per_row + b
         row = pl.ds(group, 1)
-        base = cell_ref[row, :]
+        base = wide_row(cell_ref, group, width)
         masks = z_masks(base)
         footing = jnp.concatenate(
             [ext_ref[2 * a + k, 8 * b : 8 * b + 16, :] for k in range(7)], axis=0
@@ -188,7 +195,7 @@
             along_z = along_z + weight * tilt[16 * k : 16 * k + 16]
         weight_y = rows_of_y(plain[1], group, groups, width)
         grade_y = rows_of_y(slope[1], group, groups, width)
-        minus_q = -q_ref[row, :]
+        minus_q = -wide_row(q_ref, group, width)
         pieces = (along_x * weight_y, along_y * grade_y, along_z * weight_y)
         sums = [jnp.sum(piece, axis=0, keepdims=True) for piece in pieces]
         lanes = pl.ds(pl.multiple_of(group * width, width), width)
@@ -511,7 +518,7 @@
     count = grp * pen
     slabs = len(sizes)
     starts = [sum(sizes[:s]) for s in range(slabs)]
-    groups = cell_ref.shape[0]
+    groups = off_ref.shape[1]
     block_x, block_y = KX // grp, KY // pen
     tile_rows = block_x // 2
     per_row = groups // tile_rows
@@ -539,18 +546,22 @@
         peer = lax.rem(me + d, count)
         return (peer, {"grp": lax.div(peer, pen), "pen": lax.rem(peer, pen)})
 
-    first_hop = pen * (grp // 2 - lax.rem(at_grp, grp // 2))
-
     def fan_out(make, before=None):
         def one(e, carry):
-            d = 1 + lax.rem(e + first_hop - 1, count - 1)
-            if before is not None:
-                before(d).wait_send()
-            if make is not None:
-                make(d).start()
+            plane = lax.rem(at_grp + grp + jnp.where(2 * at_grp < grp, 1 + lax.div(e, pen), -1 - lax.div(e, pen)), grp)
+            other = plane * pen + lax.rem(at_pen + lax.rem(e, pen), pen)
+            d = lax.rem(other - me + count, count)
+
+            @pl.when(d != 0)
+            def _():
+                if before is not None:
+                    before(d).wait_send()
+                if make is not None:
+                    make(d).start()
+
             return carry
 
-        lax.fori_loop(0, count - 1, one, 0)
+        lax.fori_loop(0, count, one, 0)
 
     others = pl.ds(0, count - 1)
 
@@ -851,7 +862,7 @@
 
 def whole_program(offsets, zcell, fracs, live_q, slots, grp, pen, sizes):
     count = grp * pen
-    groups, width = zcell.shape
+    groups, width = offsets.shape[1:]
     block_x, block_y = KX // grp, KY // pen
     fan = 128 // block_y
     slabs = len(sizes)
@@ -929,7 +940,11 @@
     fracs = frac.reshape(3, groups, width)
     grp, pen = lax.axis_size("grp"), lax.axis_size("pen")
     sizes = (6, 4, 4, 2)
-    if slab_fits(grp, pen, sizes, block_x, block_y, per_row):
+    if slab_fits(grp, pen, sizes, block_x, block_y, per_row) and 128 % slots == 0:
+        flat = tile_counts.reshape(-1, 128 // slots, 1)
+        alive = jnp.arange(slots, dtype=jnp.int32) < flat
+        live_q = charges.reshape(-1, 128) * alive.reshape(-1, 128).astype(jnp.float32)
+        zcell = cell_z.reshape(-1, 128)
         forces, total = whole_program(offsets, zcell, fracs, live_q, slots, grp, pen, sizes)
         return (forces, total / ATOMS)
     vmem = pl.BlockSpec(memory_space=pltpu.VMEM)

time: 143 us -> 140 us (0.979)
  Pallas kernels: 133 us -> 131 us
    pallas_call x1, Pallas kernels: 133 us -> 131 us  [whole_program(): pl.pallas_call(functools.partial(whole_kernel, grp, pen, slots, sizes), o...]
    unnamed x15 -> x13, local copies, waits for them, and re-layouts: 5.93 us -> 5.42 us
where the time goes in v7:
time: 140 us
  Pallas kernels  131 us (94%)
  local copies, waits for them, and re-layouts  5.82 us (4%)
  between operations  1.87 us (1%)
    pallas_call x1, Pallas kernels, whole_program(): pl.pallas_call(functools.partial(whole_kernel, grp, pen, slots, sizes), o...  131 us
    unnamed x13, local copies, waits for them, and re-layouts  5.42 us

profile of v7, /device:TPU:1, one launch (start us, length us, event | category | flops | bytes accessed | tf_op | source)
XLA Modules:
  0.0 139.6 jit_solution(15947632881346153163)
XLA Ops:
  0.6 0.0 copy-start.3
  0.6 0.1 lt.23
  0.7 0.6 copy-done.3
  1.3 0.1 lt.25
  1.5 0.1 copy.17
  1.5 0.0 copy-start.2
  1.6 0.0 copy-start.1
  1.6 0.1 copy.18
  1.7 0.8 copy-done.2
  2.4 0.0 copy-start
  2.5 0.7 bitcast_select_fusion.q_ref
  3.1 0.0 copy-done.1
  3.1 0.7 copy.24
  3.8 0.0 copy-done
  3.8 0.8 copy.23
  4.6 131.2 %whole.1 = (f32[3,32768]{1,0:T(4,128)}, f32[1,128]{1,0:T(1,128)}) custom-call(s32[2,128,256]{2,1,0:T(8,128)} %bitcast.15, s32[256,128]{1,0:T(8,128)} %bitcast.19, f32[3,128,256]{2,1,0:T(8,128)} %bitcast.14, f32[256,128]{1,0:T(8,128)} %bitcast_select_fusion.q_ref, bf16[256,256]{1,0:T(8,128)(2,1)} %constant.26.clone.cas_hi, ...), custom_call_target="tpu_custom_call" | custom-call | tf_op jit(solution)/shard_map/whole/pallas_call | solution.py:888
  135.9 0.0 copy-start.4
  135.9 0.6 copy-done.4
  136.5 1.9 %copy.26 = f32[3,32768]{1,0:T(4,128)} copy(f32[3,32768]{1,0:T(4,128)} %get-tuple-element.8) | data formatting | bytes 786432
  (2 shorter events, 0.0 us)
Async XLA Ops:
  0.6 0.7 copy-start.3
  1.5 0.9 copy-start.2
  1.6 1.6 %copy-start.1 = (s32[2,32768]{1,0:T(2,128)S(1)}, s32[2,32768]{1,0:T(2,128)}, u32[]{:S(2)}) copy-start(s32[2,32768]{1,0:T(2,128)} %param.15) | copy-start | bytes 786436
  2.4 1.4 copy-start
  135.9 0.6 copy-start.4
